TPU v7x, 8 devices: a whole 2x2x1 slice. The times are simulated.
8 devices in a mesh: stage: 2 (over z, y), data: 4 (over x, core).
Axes of the slice: x: 2, y: 2, z: 1, core: 2. Of those that a mesh axis runs over, the one named last changes fastest.
Arguments:
- w_master: float32 [64, 2048, 768], P('stage', 'data'), parts along dimension 0
- momentum: float32 [64, 2048, 768], P('stage', 'data'), parts along dimension 0
- grad: bfloat16 [64, 2048, 768], P('stage', 'data'), parts along dimension 0
Outputs:
- output 1: bfloat16 [64, 2048, 768], P('stage'), parts along dimension 0
- output 2: float32 [64, 2048, 768], P('stage', 'data'), parts along dimension 0
There are 2 independent parts. A program takes and returns all parts, laid end to end along the dimension named above; each array names one.
All inputs are finite; a program needn't handle non-finite values.
Results may differ from a plain program's by a relative error of at most 0.00720861.
Values are sent between devices in bfloat16 or wider.
A program may use at most 1.25 GiB of HBM per device.

v0:
```python
import math
import jax
import jax.numpy as jnp
from jax import lax
from jax.sharding import PartitionSpec as P

NS_ITERS = 5
MOMENTUM = 0.95
LEARN_RATE = 0.02
WEIGHT_DECAY = 0.1
NORM_EPS = 1e-7
COEF_A = 3.4445
COEF_B = -4.7750
COEF_C = 2.0315


def newton_schulz(x_mat):
    wide = x_mat.shape[1] <= x_mat.shape[2]
    for iteration in range(NS_ITERS):
        if wide:
            gram_mat = jnp.einsum("kip,kjp->kij", x_mat, x_mat, preferred_element_type=jnp.float32)
        else:
            gram_mat = jnp.einsum("kpi,kpj->kij", x_mat, x_mat, preferred_element_type=jnp.float32)
        gram_mat = gram_mat.astype(jnp.bfloat16)
        square = jnp.einsum("kij,kjl->kil", gram_mat, gram_mat, preferred_element_type=jnp.float32)
        poly_mat = (COEF_B * gram_mat.astype(jnp.float32) + COEF_C * square).astype(jnp.bfloat16)
        if wide:
            prod_mat = jnp.einsum("kij,kjp->kip", poly_mat, x_mat, preferred_element_type=jnp.float32)
        else:
            prod_mat = jnp.einsum("kpj,kij->kpi", x_mat, poly_mat, preferred_element_type=jnp.float32)
        x_mat = (COEF_A * x_mat.astype(jnp.float32) + prod_mat).astype(jnp.bfloat16)
    return x_mat


def solution(mesh):
    group = mesh.shape["data"]
    row_spec = P("stage", "data", None)
    full_spec = P("stage", None, None)

    def local_step(w_rows, mom_rows, grad_rows):
        mat_count, rows_dev, col_count = mom_rows.shape
        own_count = mat_count // group
        rms_scale = 0.2 * math.sqrt(max(rows_dev * group, col_count))
        mom_new = MOMENTUM * mom_rows + grad_rows.astype(jnp.float32)
        sq_total = lax.psum(jnp.sum(mom_new * mom_new, axis=(1, 2)), "data")
        owned = lax.all_to_all(mom_new.astype(jnp.bfloat16), "data", 0, 1, tiled=True)
        my_index = lax.axis_index("data")
        sq_owned = lax.dynamic_slice_in_dim(sq_total, my_index * own_count, own_count)
        x_mat = (owned.astype(jnp.float32) / (jnp.sqrt(sq_owned)[:, None, None] + NORM_EPS)).astype(jnp.bfloat16)
        x_mat = newton_schulz(x_mat)
        ortho_rows = lax.all_to_all(x_mat, "data", 1, 0, tiled=True)
        w_new = w_rows - LEARN_RATE * (ortho_rows.astype(jnp.float32) * rms_scale + WEIGHT_DECAY * w_rows)
        params = lax.all_gather(w_new.astype(jnp.bfloat16), "data", axis=1, tiled=True)
        return params, mom_new

    return jax.shard_map(local_step, mesh=mesh, in_specs=(row_spec, row_spec, row_spec), out_specs=(full_spec, row_spec), check_vma=False)
```

profile of v0, /device:TPU:0, one launch (start us, length us, event | category | flops | bytes accessed | tf_op | source)
XLA Modules:
  0.0 1910.8 jit_solution(1234062096486370613)
XLA Ops:
  7.2 40.5 %multiply_reduce_fusion = (f32[32]{0:T(128)S(1)}, f32[32,512,768]{2,1,0:T(8,128)}) fusion(bf16[32,512,768]{2,1,0:T(8,128)(2,1)} %param.5, f32[32,512,768]{2,1,0:T(8,128)} %param.4), kind=kLoop, calls=%fused_computation.12 | loop fusion | flops 62914528 | bytes 125829248 | tf_op jit(solution)/shard_map/reduce_sum | solution.py:45
  47.7 25.5 %convert_element_type.106 = bf16[32,512,768]{2,1,0:T(8,128)(2,1)} convert(f32[32,512,768]{2,1,0:T(8,128)} %get-tuple-element.7) | non-fusion elementwise | flops 12582912 | bytes 75497472 | tf_op jit(solution)/shard_map/convert_element_type | solution.py:46
  73.3 8.4 all-to-all-start
  81.7 0.0 all-gather.2.cloned.1.call-start
  81.7 274.1 %psum.7 = f32[32]{0:T(128)S(1)} all-reduce(f32[32]{0:T(128)S(1)} %get-tuple-element.2), channel_id=1, replica_groups=mesh['stage'=2,'data'=4] {'data'}, use_global_device_ids=true, to_apply=%region_1.0 | all-reduce | flops 32 | bytes 256 | tf_op jit(solution)/shard_map/psum | solution.py:45
  355.9 0.1 sqrt_add_fusion
  355.9 0.0 all-to-all-done
  355.9 27.4 %copy.12 = f32[4,8,512,768]{3,2,0,1:T(8,128)} copy(bf16[4,8,512,768]{3,2,1,0:T(8,128)(2,1)} %bitcast.6) | data formatting | bytes 75497472 | tf_op jit(solution)/shard_map/convert_element_type | solution.py:49
  383.3 26.6 %fusion = bf16[8,2048,768]{2,1,0:T(8,128)(2,1)} fusion(f32[4,8,512,768]{3,2,0,1:T(8,128)} %copy.12, f32[8]{0:T(128)S(1)} %sqrt_add_fusion), kind=kLoop, calls=%fused_computation.1 | loop fusion | flops 25165824 | bytes 75497504 | tf_op jit(solution)/shard_map/convert_element_type | solution.py:49
  409.9 31.3 %convolution_convert_fusion.4 = bf16[8,768,768]{2,1,0:T(8,128)(2,1)} fusion(bf16[8,2048,768]{2,1,0:T(8,128)(2,1)} %fusion), kind=kOutput, calls=%fused_computation.33 | convolution fusion | flops 19332071424 | bytes 34603008 | tf_op jit(solution)/shard_map/kpi,kpj->kij/dot_general | solution.py:23
  441.1 16.5 add_convert_fusion.21
  457.6 37.9 %add_convert_fusion.4 = bf16[8,2048,768]{2,1,0:T(8,128)(2,1)} fusion(bf16[8,2048,768]{2,1,0:T(8,128)(2,1)} %fusion, bf16[8,768,768]{2,1,0:T(8,128)(2,1)} %add_convert_fusion.21), kind=kOutput, calls=%fused_computation.11 | convolution fusion | flops 19377684480 | bytes 59768832 | tf_op jit(solution)/shard_map/kpj,kij->kpi/dot_general | solution.py:30
  495.6 31.3 %convolution_convert_fusion.3 = bf16[8,768,768]{2,1,0:T(8,128)(2,1)} fusion(bf16[8,2048,768]{2,1,0:T(8,128)(2,1)} %add_convert_fusion.4), kind=kOutput, calls=%fused_computation.32 | convolution fusion | flops 19332071424 | bytes 34603008 | tf_op jit(solution)/shard_map/kpi,kpj->kij/dot_general | solution.py:23
  526.9 16.7 add_convert_fusion.20
  543.6 37.6 %add_convert_fusion.3 = bf16[8,2048,768]{2,1,0:T(8,128)(2,1)} fusion(bf16[8,2048,768]{2,1,0:T(8,128)(2,1)} %add_convert_fusion.4, bf16[8,768,768]{2,1,0:T(8,128)(2,1)} %add_convert_fusion.20), kind=kOutput, calls=%fused_computation.10 | convolution fusion | flops 19377684480 | bytes 59768832 | tf_op jit(solution)/shard_map/kpj,kij->kpi/dot_general | solution.py:30
  581.2 31.5 %convolution_convert_fusion.2 = bf16[8,768,768]{2,1,0:T(8,128)(2,1)} fusion(bf16[8,2048,768]{2,1,0:T(8,128)(2,1)} %add_convert_fusion.3), kind=kOutput, calls=%fused_computation.31 | convolution fusion | flops 19332071424 | bytes 34603008 | tf_op jit(solution)/shard_map/kpi,kpj->kij/dot_general | solution.py:23
  612.7 16.5 add_convert_fusion.19
  629.2 38.2 %add_convert_fusion.2 = bf16[8,2048,768]{2,1,0:T(8,128)(2,1)} fusion(bf16[8,2048,768]{2,1,0:T(8,128)(2,1)} %add_convert_fusion.3, bf16[8,768,768]{2,1,0:T(8,128)(2,1)} %add_convert_fusion.19), kind=kOutput, calls=%fused_computation.9 | convolution fusion | flops 19377684480 | bytes 59768832 | tf_op jit(solution)/shard_map/kpj,kij->kpi/dot_general | solution.py:30
  667.4 31.3 %convolution_convert_fusion.1 = bf16[8,768,768]{2,1,0:T(8,128)(2,1)} fusion(bf16[8,2048,768]{2,1,0:T(8,128)(2,1)} %add_convert_fusion.2), kind=kOutput, calls=%fused_computation.30 | convolution fusion | flops 19332071424 | bytes 34603008 | tf_op jit(solution)/shard_map/kpi,kpj->kij/dot_general | solution.py:23
  698.8 16.6 add_convert_fusion.18
  715.4 37.6 %add_convert_fusion.1 = bf16[8,2048,768]{2,1,0:T(8,128)(2,1)} fusion(bf16[8,2048,768]{2,1,0:T(8,128)(2,1)} %add_convert_fusion.2, bf16[8,768,768]{2,1,0:T(8,128)(2,1)} %add_convert_fusion.18), kind=kOutput, calls=%fused_computation.8 | convolution fusion | flops 19377684480 | bytes 59768832 | tf_op jit(solution)/shard_map/kpj,kij->kpi/dot_general | solution.py:30
  753.0 31.5 %convolution_convert_fusion = bf16[8,768,768]{2,1,0:T(8,128)(2,1)} fusion(bf16[8,2048,768]{2,1,0:T(8,128)(2,1)} %add_convert_fusion.1), kind=kOutput, calls=%fused_computation.29 | convolution fusion | flops 19332071424 | bytes 34603008 | tf_op jit(solution)/shard_map/kpi,kpj->kij/dot_general | solution.py:23
  784.5 16.5 add_convert_fusion.17
  801.0 38.0 %add_convert_fusion = bf16[8,2048,768]{2,1,0:T(8,128)(2,1)} fusion(bf16[8,2048,768]{2,1,0:T(8,128)(2,1)} %add_convert_fusion.1, bf16[8,768,768]{2,1,0:T(8,128)(2,1)} %add_convert_fusion.17), kind=kOutput, calls=%fused_computation.7 | convolution fusion | flops 19377684480 | bytes 59768832 | tf_op jit(solution)/shard_map/kpj,kij->kpi/dot_general | solution.py:30
  839.0 23.2 %copy.18 = bf16[8,2048,768]{2,0,1:T(8,128)(2,1)S(1)} copy(bf16[8,2048,768]{2,1,0:T(8,128)(2,1)} %add_convert_fusion) | data formatting | bytes 50331648 | tf_op jit(solution)/shard_map/convert_element_type | solution.py:31
  862.2 277.8 %all_to_all.8 = bf16[8,2048,768]{2,0,1:T(8,128)(2,1)} all-to-all(bf16[8,2048,768]{2,0,1:T(8,128)(2,1)S(1)} %copy.18), channel_id=1, replica_groups=mesh['stage'=2,'data'=4] {'data'}, dimensions={1} | all-to-all | bytes 50331648 | tf_op jit(solution)/shard_map/all_to_all | solution.py:51
  1140.1 27.4 %convert_multiply_fusion = f32[8,2048,768]{2,0,1:T(8,128)} fusion(bf16[8,2048,768]{2,0,1:T(8,128)(2,1)} %all_to_all.8), kind=kLoop, calls=%fused_computation.6 | loop fusion | flops 25165824 | bytes 75497472 | tf_op jit(solution)/shard_map/mul | solution.py:52
  1167.5 45.5 %copy.19 = f32[4,8,512,768]{3,2,1,0:T(8,128)} copy(f32[4,8,512,768]{3,1,2,0:T(8,128)} %bitcast.64) | data formatting | bytes 100663296 | tf_op jit(solution)/shard_map/mul | solution.py:52
  1213.0 40.6 %fusion.3 = bf16[32,512,768]{2,1,0:T(8,128)(2,1)} fusion(f32[32,512,768]{2,1,0:T(8,128)} %param.3, f32[4,8,512,768]{3,2,1,0:T(8,128)} %copy.19), kind=kLoop, calls=%fused_computation.5 | loop fusion | flops 62914560 | bytes 125829120 | tf_op jit(solution)/shard_map/convert_element_type | solution.py:53
  1253.6 0.0 all-gather.2.cloned.1.call-update
  1253.6 583.3 %all-gather.2.cloned.1.call-done = bf16[32,2048,768]{2,1,0:T(8,128)(2,1)} async-done(((bf16[32,512,768]{2,1,0:T(8,128)(2,1)}), bf16[32,2048,768]{2,1,0:T(8,128)(2,1)}) %all-gather.2.cloned.1.call-update) | async-done | bytes 100663312 | tf_op jit(solution)/shard_map/all_gather | solution.py:53
  1836.9 66.6 %copy.26 = bf16[32,2048,768]{2,1,0:T(8,128)(2,1)} copy(bf16[32,2048,768]{2,1,0:T(8,128)(2,1)} %all-gather.2.cloned.1.call-done) | data formatting | bytes 201326592
Async XLA Ops:
  73.3 282.7 %all-to-all-start = ((bf16[32,512,768]{2,1,0:T(8,128)(2,1)}), bf16[32,512,768]{2,1,0:T(8,128)(2,1)}, u32[]{:S(2)}, u32[]{:S(2)}) async-start(bf16[32,512,768]{2,1,0:T(8,128)(2,1)} %convert_element_type.106), calls=%async_computation | async-start | bytes 50331648 | tf_op jit(solution)/shard_map/all_to_all | solution.py:46
  81.7 1755.3 %all-gather.2.cloned.1.call-start = ((), (), s32[]{:S(2)}) async-start(), calls=%async_computation.2 | async-start | bytes 125829120 | tf_op jit(solution)/shard_map/all_gather | solution.py:53
Sparse Core Ops, SparseCore 0:
  1253.8 583.1 all-gather.1
where the time goes:
time: 1920 us; the launch traced here: 1910 us
  waiting for transfers between devices  583 us (30%)
  blocking collectives  552 us (29%)
  matrix products  429 us (22%)
  local copies, waits for them, and re-layouts  163 us (8%)
  other arithmetic  161 us (8%)
    all_gather x1, waiting for transfers between devices, local_step(): lax.all_gather(w_new.astype(jnp.bfloat16), 'data', axis=1, tiled=True)  583 us
    all_to_all x1, blocking collectives, local_step(): ortho_rows = lax.all_to_all(x_mat, 'data', 1, 0, tiled=True)  278 us
    psum x1, blocking collectives, local_step(): sq_total = lax.psum(jnp.sum(mom_new * mom_new, axis=(1, 2)), 'data')  274 us
    dot_general x5, matrix products, newton_schulz(): jnp.einsum('kpj,kij->kpi', x_mat, poly_mat, preferred_element_type=jnp.fl...  189 us
    dot_general x5, matrix products, newton_schulz(): jnp.einsum('kpi,kpj->kij', x_mat, x_mat, preferred_element_type=jnp.float32)  157 us
    dot_general x5, matrix products, newton_schulz(): jnp.einsum('kij,kjl->kil', gram_mat, gram_mat, preferred_element_type=jnp...  82.8 us
    unnamed x1, local copies, waits for them, and re-layouts  66.6 us
    mul x1, local copies, waits for them, and re-layouts, local_step(): ortho_rows.astype(jnp.float32) * rms_scale + WEIGHT_DECAY * w_rows  45.5 us
  transfers between devices with their start and end apart: 2, of which 1 were waited for; matrix products, arithmetic and copies ran while one was open for 0% of the time, Pallas kernels for 0%

commit v1 on v0

v1 whole, which is shorter than its diff:
```python
import functools
import math

import jax
import jax.numpy as jnp
from jax import lax
from jax.experimental import pallas as pl
from jax.experimental.pallas import tpu as pltpu
from jax.sharding import PartitionSpec as P


NS_ITERS = 5
MOMENTUM = 0.95
LEARN_RATE = 0.02
WEIGHT_DECAY = 0.1
NORM_EPS = 1e-7
COEF_A = 3.4445
COEF_B = -4.7750
COEF_C = 2.0315

GROUP = 4
CHUNKS = (1, 7, 8, 8, 4, 2, 1, 1)
FIRSTS = tuple(sum(CHUNKS[:c]) for c in range(len(CHUNKS)))
ORDER = (2, 3, 1, 0)
X_PERM = ((0, 2), (1, 3), (2, 0), (3, 1))
CORE_PERM = ((0, 1), (1, 0), (2, 3), (3, 2))


def relations(me):
    partner = me + 1 - 2 * lax.rem(me, 2)
    return me, partner, lax.rem(me + 2, GROUP), lax.rem(partner + 2, GROUP)


def exchange_kernel(rounds, rms_scale, w_ref, mom_ref, grad_ref, *refs):
    n = len(CHUNKS)
    w_outs, (w_chip, mb, xin, oo, orv) = refs[:n], refs[n : n + 5]
    (fbuf, hbuf, sbuf, ss_loc, ss_in, xa, xb, amat, bmat, f_sem, h_sem, st_sem, x_sem,
     m_send, m_recv, s_send, s_recv, o_send, o_recv, w_send, w_recv) = refs[n + 5 :]
    rows, cols = mom_ref.shape[1], mom_ref.shape[2]
    rel = relations(lax.axis_index("data"))
    strip = 64

    barrier = pltpu.get_barrier_semaphore()
    for k in (1, 2, 3):
        pl.semaphore_signal(barrier, inc=1, device_id={"data": rel[k]}, device_id_type=pl.DeviceIdType.MESH)
    pl.semaphore_wait(barrier, GROUP - 1)

    def remote(src, dst, send, recv, k):
        return pltpu.make_async_remote_copy(
            src_ref=src, dst_ref=dst, send_sem=send, recv_sem=recv,
            device_id={"data": rel[k]}, device_id_type=pl.DeviceIdType.MESH)

    def load_m(r, k, slot):
        m = GROUP * r + rel[k]
        return (pltpu.make_async_copy(mom_ref.at[m], fbuf.at[slot], f_sem.at[slot]),
                pltpu.make_async_copy(grad_ref.at[m], hbuf.at[slot], h_sem.at[slot]))

    def stage_m(r, k, slot):
        dst = xin.at[r, pl.ds(0, rows)] if k == 0 else mb.at[r, k - 1]
        return pltpu.make_async_copy(sbuf.at[slot], dst, st_sem.at[slot])

    def send_m(r, k):
        return (remote(mb.at[r, k - 1], xin.at[r, pl.ds(k * rows, rows)], m_send.at[r, k - 1], m_recv.at[r, k - 1], k),
                remote(ss_loc.at[r, k - 1], ss_in.at[r, k], s_send.at[r, k - 1], s_recv.at[r, k - 1], k))

    for copy in load_m(0, ORDER[0], 0):
        copy.start()

    def momentum_round(r, carry):
        for j, k in enumerate(ORDER):
            slot = j % 2
            for copy in load_m(r, k, slot):
                copy.wait()
            if j + 1 < GROUP:
                for copy in load_m(r, ORDER[j + 1], 1 - slot):
                    copy.start()
            else:
                @pl.when(r + 1 < rounds)
                def _():
                    for copy in load_m(r + 1, ORDER[0], 1 - slot):
                        copy.start()

            def part(i, acc):
                sl = pl.ds(pl.multiple_of(i * strip, strip), strip)
                mom_new = MOMENTUM * fbuf[slot, sl, :] + hbuf[slot, sl, :].astype(jnp.float32)
                sbuf[slot, sl, :] = mom_new.astype(jnp.bfloat16)
                return acc + jnp.sum((mom_new * mom_new).reshape(strip // 8, 8, cols), axis=0)

            acc = lax.fori_loop(0, rows // strip, part, jnp.zeros((8, cols), jnp.float32))
            total = jnp.broadcast_to(jnp.sum(jnp.sum(acc, axis=0, keepdims=True), axis=1, keepdims=True), (8, 128))
            if k == 0:
                ss_in[r, 0] = total
            else:
                ss_loc[r, k - 1] = total
            stage_m(r, k, slot).start()
            if j > 0:
                before = ORDER[j - 1]
                stage_m(r, before, 1 - slot).wait()
                for copy in send_m(r, before):
                    copy.start()
            else:
                @pl.when(r > 0)
                def _():
                    stage_m(r - 1, ORDER[-1], 1 - slot).wait()
        return carry

    lax.fori_loop(0, rounds, momentum_round, 0)
    stage_m(rounds - 1, ORDER[-1], (GROUP - 1) % 2).wait()

    def send_o(r, k):
        return remote(oo.at[r, pl.ds(k * rows, rows)], orv.at[r, rel[0]], o_send.at[r, k - 1], o_recv.at[r, k - 1], k)

    def ortho_round(r, carry):
        for k in (1, 2, 3):
            for copy in send_m(r, k):
                copy.wait_recv()
        fetch = pltpu.make_async_copy(xin.at[r], xa, x_sem)
        fetch.start()
        fetch.wait()
        total = ss_in[r, 0] + ss_in[r, 1] + ss_in[r, 2] + ss_in[r, 3]
        denom = (jnp.sqrt(total) + NORM_EPS)[0:1, 0:1]

        def scale(i, c):
            sl = pl.ds(pl.multiple_of(i * strip, strip), strip)
            xb[sl, :] = (xa[sl, :].astype(jnp.float32) / denom).astype(jnp.bfloat16)
            return c

        lax.fori_loop(0, GROUP * rows // strip, scale, 0)

        def iterate(_, c):
            x_mat = xb[...]
            amat[...] = lax.dot_general(x_mat, x_mat, (((0,), (0,)), ((), ())),
                                        preferred_element_type=jnp.float32).astype(jnp.bfloat16)
            a_mat = amat[...]
            square = jnp.dot(a_mat, a_mat, preferred_element_type=jnp.float32)
            bmat[...] = (COEF_B * a_mat.astype(jnp.float32) + COEF_C * square).astype(jnp.bfloat16)

            def update(i, c2):
                sl = pl.ds(pl.multiple_of(i * rows, rows), rows)
                x_rows = xb[sl, :]
                prod = jnp.dot(x_rows, bmat[...], preferred_element_type=jnp.float32)
                xb[sl, :] = (COEF_A * x_rows.astype(jnp.float32) + prod).astype(jnp.bfloat16)
                return c2

            return lax.fori_loop(0, GROUP, update, c)

        lax.fori_loop(0, NS_ITERS, iterate, 0)
        kept = pltpu.make_async_copy(xb.at[pl.ds(0, rows)], orv.at[r, rel[0]], f_sem.at[0])
        out = pltpu.make_async_copy(xb, oo.at[r], x_sem)
        out.start()
        kept.start()
        out.wait()
        for k in ORDER[:3]:
            send_o(r, k).start()
        kept.wait()
        return carry

    lax.fori_loop(0, rounds, ortho_round, 0)

    def load_w(m, slot):
        return (pltpu.make_async_copy(w_ref.at[m], fbuf.at[slot], f_sem.at[slot]),
                pltpu.make_async_copy(orv.at[m // GROUP, lax.rem(m, GROUP)], hbuf.at[slot], h_sem.at[slot]))

    def load_round(m, slot):
        for k in (1, 2, 3):
            send_o(m // GROUP, k).wait_recv()
        for copy in load_w(m, slot):
            copy.start()

    def stage_w(c, i, slot):
        return pltpu.make_async_copy(sbuf.at[slot], w_outs[c].at[i], st_sem.at[slot])

    def send_w(i):
        return remote(w_outs[0].at[i], w_chip.at[i], w_send.at[i], w_recv.at[i], 2)

    mats = GROUP * rounds
    load_round(0, 0)

    def weights(m, carry):
        slot, later = lax.rem(m, 2), m + 1
        for copy in load_w(m, slot):
            copy.wait()

        @pl.when(lax.rem(later, GROUP) != 0)
        def _():
            for copy in load_w(later, 1 - slot):
                copy.start()

        @pl.when(m >= 2)
        def _():
            stage_w(0, 0, slot).wait()

        @pl.when(m == CHUNKS[0] + 1)
        def _():
            for i in range(CHUNKS[0]):
                send_w(i).start()

        def part(i, c):
            sl = pl.ds(pl.multiple_of(i * strip, strip), strip)
            w_old = fbuf[slot, sl, :]
            ortho = hbuf[slot, sl, :].astype(jnp.float32) * rms_scale
            sbuf[slot, sl, :] = (w_old - LEARN_RATE * (ortho + WEIGHT_DECAY * w_old)).astype(jnp.bfloat16)
            return c

        lax.fori_loop(0, rows // strip, part, 0)
        for c in range(n):
            @pl.when((m >= FIRSTS[c]) & (m < FIRSTS[c] + CHUNKS[c]))
            def _():
                stage_w(c, m - FIRSTS[c], slot).start()

        @pl.when((lax.rem(later, GROUP) == 0) & (later < mats))
        def _():
            load_round(later, 1 - slot)

        return carry

    lax.fori_loop(0, mats, weights, 0)
    stage_w(0, 0, 0).wait()
    stage_w(0, 0, 1).wait()
    for i in range(CHUNKS[0]):
        send_w(i).wait()

    def drain(r, carry):
        for k in (1, 2, 3):
            for copy in send_m(r, k):
                copy.wait_send()
            send_o(r, k).wait_send()
        return carry

    lax.fori_loop(0, rounds, drain, 0)


def exchange(w_rows, mom_rows, grad_rows):
    mats, rows, cols = mom_rows.shape
    rounds = mats // GROUP
    half, full = jnp.bfloat16, jnp.float32
    rms_scale = 0.2 * math.sqrt(max(rows * GROUP, cols))
    shapes = [jax.ShapeDtypeStruct((count, rows, cols), half) for count in CHUNKS + CHUNKS[:1]] + [
        jax.ShapeDtypeStruct((rounds, 3, rows, cols), half),
        jax.ShapeDtypeStruct((rounds, GROUP * rows, cols), half),
        jax.ShapeDtypeStruct((rounds, GROUP * rows, cols), half),
        jax.ShapeDtypeStruct((rounds, GROUP, rows, cols), half),
    ]
    dma = pltpu.SemaphoreType.DMA
    flops = rounds * NS_ITERS * 2 * cols * cols * (2 * rows * GROUP + cols)
    outs = pl.pallas_call(
        functools.partial(exchange_kernel, rounds, rms_scale),
        out_shape=shapes,
        in_specs=[pl.BlockSpec(memory_space=pltpu.HBM)] * 3,
        out_specs=[pl.BlockSpec(memory_space=pltpu.HBM)] * len(shapes),
        scratch_shapes=[
            pltpu.VMEM((2, rows, cols), full),
            pltpu.VMEM((2, rows, cols), half),
            pltpu.VMEM((2, rows, cols), half),
            pltpu.VMEM((rounds, 3, 8, 128), full),
            pltpu.VMEM((rounds, GROUP, 8, 128), full),
            pltpu.VMEM((GROUP * rows, cols), half),
            pltpu.VMEM((GROUP * rows, cols), half),
            pltpu.VMEM((cols, cols), half),
            pltpu.VMEM((cols, cols), half),
            dma((2,)), dma((2,)), dma((2,)), dma,
            *[dma((rounds, 3))] * 6, *[dma((CHUNKS[0],))] * 2,
        ],
        compiler_params=pltpu.CompilerParams(collective_id=0, has_side_effects=True, vmem_limit_bytes=60 * 1024 * 1024),
        cost_estimate=pl.CostEstimate(flops=flops, bytes_accessed=12 * mats * rows * cols, transcendentals=0),
        name="exchange",
    )(w_rows, mom_rows, grad_rows)
    return outs[: len(CHUNKS)], outs[len(CHUNKS)]


def place_kernel(first, parts, *refs):
    blocks, (out_ref, buf, in_sem, out_sem) = refs[: len(parts)], refs[-4:]
    count, rows, _ = blocks[0].shape
    rel = relations(lax.axis_index("data"))

    def fetch(i, n, slot):
        return pltpu.make_async_copy(blocks[n].at[i], buf.at[slot, n], in_sem.at[slot, n])

    def put(i, n, slot):
        dst = out_ref.at[first + i, pl.ds(pl.multiple_of(rel[parts[n]] * rows, rows), rows)]
        return pltpu.make_async_copy(buf.at[slot, n], dst, out_sem.at[slot, n])

    for n in range(len(parts)):
        fetch(0, n, 0).start()

    def step(i, carry):
        slot = lax.rem(i, 2)
        for n in range(len(parts)):
            @pl.when(i >= 1)
            def _():
                put(i - 1, n, 1 - slot).wait()

            @pl.when(i + 1 < count)
            def _():
                fetch(i + 1, n, 1 - slot).start()

        for n in range(len(parts)):
            fetch(i, n, slot).wait()
            put(i, n, slot).start()
        return carry

    lax.fori_loop(0, count, step, 0)
    for n in range(len(parts)):
        put(count - 1, n, (count - 1) % 2).wait()


def place(chunk, blocks, dst, mats):
    parts = tuple(blocks)
    count, rows, cols = blocks[parts[0]].shape
    args, aliases = [blocks[k] for k in parts], {}
    if dst is not None:
        aliases = {len(args): 0}
        args.append(dst)
    size = len(parts) * count * rows * cols
    dma = pltpu.SemaphoreType.DMA
    return pl.pallas_call(
        functools.partial(place_kernel, FIRSTS[chunk], parts),
        out_shape=jax.ShapeDtypeStruct((mats, rows * GROUP, cols), jnp.bfloat16),
        in_specs=[pl.BlockSpec(memory_space=pltpu.HBM)] * len(args),
        out_specs=pl.BlockSpec(memory_space=pltpu.HBM),
        scratch_shapes=[pltpu.VMEM((2, len(parts), rows, cols), jnp.bfloat16), dma((2, len(parts))), dma((2, len(parts)))],
        input_output_aliases=aliases,
        cost_estimate=pl.CostEstimate(flops=size, bytes_accessed=4 * size, transcendentals=0),
        name="place",
    )(*args)


def solution(mesh):
    row_spec = P("stage", "data", None)
    full_spec = P("stage", None, None)
    last = len(CHUNKS) - 1

    def local_step(w_rows, mom_rows, grad_rows):
        mats = mom_rows.shape[0]
        own, w_chip = exchange(w_rows, mom_rows, grad_rows)
        chip, core, diag = [w_chip], [], []
        for c in range(1, last + 1):
            chip.append(lax.ppermute(own[c], "data", X_PERM))
        for c in range(last + 1):
            core.append(lax.ppermute(own[c], "data", CORE_PERM))
            diag.append(lax.ppermute(chip[c], "data", CORE_PERM))
        mom_late, grad_late, _ = lax.optimization_barrier((mom_rows, grad_rows, own[0]))
        mom_new = MOMENTUM * mom_late + grad_late.astype(jnp.float32)
        params = None
        for c in range(last):
            params = place(c, {0: own[c], 1: core[c], 2: chip[c], 3: diag[c]}, params, mats)
        params = place(last, {0: own[last], 1: core[last], 2: chip[last]}, params, mats)
        params = place(last, {3: diag[last]}, params, mats)
        return params, mom_new

    return jax.shard_map(local_step, mesh=mesh, in_specs=(row_spec, row_spec, row_spec), out_specs=(full_spec, row_spec), check_vma=False)
```

time: 1920 us -> 1270 us (0.66)
  Pallas kernels: 0 us -> 645 us
  blocking collectives: 552 us -> 0 us
  matrix products: 429 us -> 0 us
  local copies, waits for them, and re-layouts: 163 us -> 10.2 us
  other arithmetic: 161 us -> 41.3 us
  waiting for transfers between devices: 583 us -> 555 us
    pallas_call x0 -> x10, Pallas kernels: none -> 645 us  [the longest x1 568 us: exchange(): pl.pallas_call(functools.partial(exchange_kernel, rounds, rms_scale), out...]
    all_gather x1 -> x0, waiting for transfers between devices: 583 us -> none  [local_step(): lax.all_gather(w_new.astype(jnp.bfloat16), 'data', axis=1, tiled=True)]
    ppermute x0 -> x23, waiting for transfers between devices: none -> 555 us  [the longest x7 518 us: local_step(): chip.append(lax.ppermute(own[c], 'data', X_PERM))]
    dot_general x15 -> x0, matrix products: 429 us -> none  [the longest x5 189 us: newton_schulz(): jnp.einsum('kpj,kij->kpi', x_mat, poly_mat, preferred_element_type=jnp.fl...]
    all_to_all x1 -> x0, blocking collectives: 278 us -> none  [local_step(): ortho_rows = lax.all_to_all(x_mat, 'data', 1, 0, tiled=True)]
    psum x1 -> x0, blocking collectives: 274 us -> none  [local_step(): sq_total = lax.psum(jnp.sum(mom_new * mom_new, axis=(1, 2)), 'data')]
    convert_element_type x3 -> x0, other arithmetic: 92.7 us -> none  [the longest x1 40.6 us: local_step(): w_new.astype(jnp.bfloat16)]
    unnamed x1 -> x30, local copies, waits for them, and re-layouts: 66.6 us -> 10.2 us
  transfers between devices with their start and end apart: 2 -> 23, of which waited for: 1 -> 5; matrix products, arithmetic and copies ran while one was open for 0% -> 3% of each run, Pallas kernels for 0% -> 6%
where the time goes in v1:
time: 1270 us; the launch traced here: 1260 us
  Pallas kernels  645 us (51%)
  waiting for transfers between devices  555 us (44%)
  other arithmetic  41.3 us (3%)
    pallas_call x1, Pallas kernels, exchange(): pl.pallas_call(functools.partial(exchange_kernel, rounds, rms_scale), out...  568 us
    ppermute x7, waiting for transfers between devices, local_step(): chip.append(lax.ppermute(own[c], 'data', X_PERM))  518 us
    pallas_call x9, Pallas kernels, place(): pl.pallas_call(functools.partial(place_kernel, FIRSTS[chunk], parts), out...  77 us
    add x1, other arithmetic, local_step(): mom_new = MOMENTUM * mom_late + grad_late.astype(jnp.float32)  41.3 us
    ppermute x8, waiting for transfers between devices, local_step(): diag.append(lax.ppermute(chip[c], 'data', CORE_PERM))  30.2 us
  transfers between devices with their start and end apart: 23, of which 5 were waited for; matrix products, arithmetic and copies ran while one was open for 3% of the time, Pallas kernels for 6%

profile of v1, /device:TPU:0, one launch (start us, length us, event | category | flops | bytes accessed | tf_op | source)
XLA Modules:
  0.0 1264.1 jit_solution(3471592954995562218)
XLA Ops:
  0.6 568.0 %exchange.1 = (bf16[1,512,768]{2,1,0:T(8,128)(2,1)}, bf16[7,512,768]{2,1,0:T(8,128)(2,1)}, bf16[8,512,768]{2,1,0:T(8,128)(2,1)}, bf16[8,512,768]{2,1,0:T(8,128)(...) custom-call(f32[32,512,768]{2,1,0:T(8,128)} %w_ref.1, ...), custom_call_target="tpu_custom_call" | custom-call | flops 229512314880 | bytes 150994944 | tf_op jit(solution)/shard_map/exchange/pallas_call | solution.py:246
  568.6 0.0 collective-permute-start.21
  568.6 0.5 collective-permute-start.22
  569.1 1.6 collective-permute-start.10
  570.8 0.4 collective-permute-start.7
  571.2 0.0 collective-permute-start.6
  571.2 0.0 collective-permute-done.21.refs_1_
  571.2 1.7 collective-permute-start.4
  572.8 0.0 collective-permute-done.22.refs_3_
  572.8 1.0 collective-permute-start
  573.9 117.1 %collective-permute-done.4.refs_2_ = bf16[1,512,768]{2,1,0:T(8,128)(2,1)} collective-permute-done((bf16[1,512,768]{2,1,0:T(8,128)(2,1)}, bf16[1,512,768]{2,1,0:T(8,128)(2,1)}, u32[]{:S(2)}, u32[]{:S(2)}) %collective-permute-start.4) | collective-permute-done | bytes 786464 | tf_op jit(solution)/shard_map/ppermute | solution.py:338
  691.0 0.0 collective-permute-start.9
  691.0 15.9 %collective-permute-done.refs_2_ = bf16[1,512,768]{2,1,0:T(8,128)(2,1)} collective-permute-done((bf16[1,512,768]{2,1,0:T(8,128)(2,1)}, bf16[1,512,768]{2,1,0:T(8,128)(2,1)}, u32[]{:S(2)}, u32[]{:S(2)}) %collective-permute-start) | collective-permute-done | bytes 786464 | tf_op jit(solution)/shard_map/ppermute | solution.py:338
  706.9 1.6 collective-permute-start.16
  708.5 0.0 collective-permute-done.7.refs_2_
  708.5 0.4 collective-permute-start.13
  708.9 0.0 collective-permute-done.6.refs_1_
  708.9 1.6 collective-permute-start.19
  710.6 0.0 collective-permute-done.10.refs_2_
  710.6 0.0 collective-permute-start.18
  710.6 0.0 collective-permute-done.9.refs_1_
  710.6 0.5 collective-permute-start.15
  711.1 385.4 %collective-permute-done.19.refs_2_ = bf16[7,512,768]{2,1,0:T(8,128)(2,1)S(1)} collective-permute-done((bf16[7,512,768]{2,1,0:T(8,128)(2,1)}, bf16[7,512,768]{2,1,0:T(8,128)(2,1)S(1)}, u32[]{:S(2)}, u32[]{:S(2)}) %collective-permute-start.19) | collective-permute-done | bytes 5505056 | tf_op jit(solution)/shard_map/ppermute | solution.py:338
  1096.5 0.0 collective-permute-start.12
  1096.5 0.0 collective-permute-done.16.refs_2_
  1096.5 2.6 copy-done
  1099.2 0.5 collective-permute-start.17
  1099.6 0.0 collective-permute-done.13.refs_2_
  1099.6 0.0 collective-permute-start.14
  1099.7 0.0 copy-done.12
  1099.7 0.0 collective-permute-done.18.refs_1_
  1099.7 0.5 collective-permute-start.20
  1100.2 0.0 collective-permute-done.15.refs_1_
  1100.2 0.0 collective-permute-start.11
  1100.2 6.6 collective-permute-done.12.refs_1_
  1106.9 0.1 collective-permute-start.3
  1107.0 30.2 %collective-permute-done.11.refs_3_ = bf16[4,512,768]{2,1,0:T(8,128)(2,1)S(1)} collective-permute-done((bf16[4,512,768]{2,1,0:T(8,128)(2,1)S(1)}, bf16[4,512,768]{2,1,0:T(8,128)(2,1)S(1)}, u32[]{:S(2)}, u32[]{:S(2)}) %collective-permute-start.11) | collective-permute-done | bytes 3145760 | tf_op jit(solution)/shard_map/ppermute | solution.py:341
  1137.2 0.1 collective-permute-start.2
  1137.4 0.0 collective-permute-done.20.refs_3_
  1137.4 0.4 collective-permute-start.5
  1137.8 0.0 collective-permute-done.17.refs_3_
  1137.8 0.2 collective-permute-start.1
  1137.9 0.0 collective-permute-done.14.refs_3_
  1137.9 0.0 copy-done.7
  1138.0 1.0 copy-done.11
  1139.0 1.6 copy-done.8
  1140.6 2.1 copy-done.4
  1142.7 2.7 copy-done.5
  1145.4 0.1 collective-permute-start.8
  1145.6 41.3 %convert_add_fusion = f32[32,512,768]{2,1,0:T(8,128)} fusion(bf16[32,512,768]{2,1,0:T(8,128)(2,1)} %grad_ref.1, f32[32,512,768]{2,1,0:T(8,128)} %mom_ref.1), kind=kLoop, calls=%fused_computation | loop fusion | flops 37748736 | bytes 125829120 | tf_op jit(solution)/shard_map/add | solution.py:343
  1186.9 2.9 place.9.refs_4_
  1189.9 15.4 %place.10.refs_4_ = bf16[32,2048,768]{2,1,0:T(8,128)(2,1)} custom-call(bf16[7,512,768]{2,1,0:T(8,128)(2,1)} %get-tuple-element.19.refs_0_, bf16[7,512,768]{2,1,0:T(8,128)(2,1)} %copy-done.7, bf16[7,512,768]{2,1,0:T(8,128)(2,1)} %copy-done.6, bf16[7,512,768]{2,1,0:T(8,128)(2,1)} %copy-done.8, ...), custom_call_target="tpu_custom_call", output_to_operand_aliasing={{}: (4, {})} | custom-call | flops 11010048 | bytes 44040192 | tf_op jit(solution)/shard_map/place/pallas_call | solution.py:316
  1205.3 18.0 %place.11.refs_4_ = bf16[32,2048,768]{2,1,0:T(8,128)(2,1)} custom-call(bf16[8,512,768]{2,1,0:T(8,128)(2,1)} %get-tuple-element.18.refs_0_, bf16[8,512,768]{2,1,0:T(8,128)(2,1)} %copy-done.2, bf16[8,512,768]{2,1,0:T(8,128)(2,1)} %copy-done, bf16[8,512,768]{2,1,0:T(8,128)(2,1)} %copy-done.4, ...), custom_call_target="tpu_custom_call", output_to_operand_aliasing={{}: (4, {})} | custom-call | flops 12582912 | bytes 50331648 | tf_op jit(solution)/shard_map/place/pallas_call | solution.py:316
  1223.3 18.0 %place.12.refs_4_ = bf16[32,2048,768]{2,1,0:T(8,128)(2,1)} custom-call(bf16[8,512,768]{2,1,0:T(8,128)(2,1)} %get-tuple-element.17.refs_0_, bf16[8,512,768]{2,1,0:T(8,128)(2,1)} %copy-done.3, bf16[8,512,768]{2,1,0:T(8,128)(2,1)} %copy-done.1, bf16[8,512,768]{2,1,0:T(8,128)(2,1)} %copy-done.5, ...), custom_call_target="tpu_custom_call", output_to_operand_aliasing={{}: (4, {})} | custom-call | flops 12582912 | bytes 50331648 | tf_op jit(solution)/shard_map/place/pallas_call | solution.py:316
  1241.3 9.6 place.13.refs_4_
  1250.9 0.0 collective-permute-done.8.refs_3_
  1250.9 5.5 place.14.refs_4_
  1256.4 0.0 collective-permute-done.3.refs_1_
  1256.4 0.0 collective-permute-done.5.refs_3_
  1256.4 2.9 place.15.refs_3_
  1259.4 0.0 collective-permute-done.2.refs_1_
  1259.4 2.6 place.16.refs_1_
  1262.0 0.0 collective-permute-done.1.refs_0_
  1262.0 2.1 place.17
  (23 shorter events, 0.0 us)
Async XLA Ops:
  568.6 2.6 collective-permute-start.21
  568.6 4.2 collective-permute-start.22
  569.1 141.4 %collective-permute-start.10 = (bf16[4,512,768]{2,1,0:T(8,128)(2,1)}, bf16[4,512,768]{2,1,0:T(8,128)(2,1)S(1)}, u32[]{:S(2)}, u32[]{:S(2)}) collective-permute-start(bf16[4,512,768]{2,1,0:T(8,128)(2,1)} %get-tuple-element.16.refs_0_), channel_id=1, source_target_pairs={{0,2},{1,3},{2,0},{3,1},{4,6},{5,7},{6,4},{7,5}} | collective-permute-start | bytes 9437192 | tf_op jit(solution)/shard_map/ppermute | solution.py:338
  570.8 137.8 %collective-permute-start.7 = (bf16[2,512,768]{2,1,0:T(8,128)(2,1)}, bf16[2,512,768]{2,1,0:T(8,128)(2,1)}, u32[]{:S(2)}, u32[]{:S(2)}) collective-permute-start(bf16[2,512,768]{2,1,0:T(8,128)(2,1)} %get-tuple-element.15.refs_0_), channel_id=1, source_target_pairs={{0,2},{1,3},{2,0},{3,1},{4,6},{5,7},{6,4},{7,5}} | collective-permute-start | bytes 4718600 | tf_op jit(solution)/shard_map/ppermute | solution.py:338
  571.2 137.8 %collective-permute-start.6 = (bf16[2,512,768]{2,1,0:T(8,128)(2,1)}, bf16[2,512,768]{2,1,0:T(8,128)(2,1)S(1)}, u32[]{:S(2)}, u32[]{:S(2)}) collective-permute-start(bf16[2,512,768]{2,1,0:T(8,128)(2,1)} %get-tuple-element.15.refs_0_), channel_id=1, source_target_pairs={{0,1},{1,0},{2,3},{3,2},{4,5},{5,4},{6,7},{7,6}} | collective-permute-start | bytes 4718600 | tf_op jit(solution)/shard_map/ppermute | solution.py:340
  571.2 615.8 %copy-start.13 = (bf16[1,512,768]{2,1,0:T(8,128)(2,1)}, bf16[1,512,768]{2,1,0:T(8,128)(2,1)S(1)}, u32[]{:S(2)}) copy-start(bf16[1,512,768]{2,1,0:T(8,128)(2,1)S(1)} %collective-permute-done.21.refs_1_) | copy-start | bytes 2359300
  571.2 119.8 %collective-permute-start.4 = (bf16[1,512,768]{2,1,0:T(8,128)(2,1)}, bf16[1,512,768]{2,1,0:T(8,128)(2,1)}, u32[]{:S(2)}, u32[]{:S(2)}) collective-permute-start(bf16[1,512,768]{2,1,0:T(8,128)(2,1)} %get-tuple-element.14.refs_0_), channel_id=1, source_target_pairs={{0,2},{1,3},{2,0},{3,1},{4,6},{5,7},{6,4},{7,5}} | collective-permute-start | bytes 2359304 | tf_op jit(solution)/shard_map/ppermute | solution.py:338
  572.8 614.1 %copy-start.14 = (bf16[1,512,768]{2,1,0:T(8,128)(2,1)}, bf16[1,512,768]{2,1,0:T(8,128)(2,1)S(1)}, u32[]{:S(2)}) copy-start(bf16[1,512,768]{2,1,0:T(8,128)(2,1)S(1)} %collective-permute-done.22.refs_3_) | copy-start | bytes 2359300
  572.8 134.1 %collective-permute-start = (bf16[1,512,768]{2,1,0:T(8,128)(2,1)}, bf16[1,512,768]{2,1,0:T(8,128)(2,1)}, u32[]{:S(2)}, u32[]{:S(2)}) collective-permute-start(bf16[1,512,768]{2,1,0:T(8,128)(2,1)} %get-tuple-element.13.refs_0_), channel_id=1, source_target_pairs={{0,2},{1,3},{2,0},{3,1},{4,6},{5,7},{6,4},{7,5}} | collective-permute-start | bytes 2359304 | tf_op jit(solution)/shard_map/ppermute | solution.py:338
  691.0 19.6 %collective-permute-start.9 = (bf16[4,512,768]{2,1,0:T(8,128)(2,1)}, bf16[4,512,768]{2,1,0:T(8,128)(2,1)S(1)}, u32[]{:S(2)}, u32[]{:S(2)}) collective-permute-start(bf16[4,512,768]{2,1,0:T(8,128)(2,1)} %get-tuple-element.16.refs_0_), channel_id=1, source_target_pairs={{0,1},{1,0},{2,3},{3,2},{4,5},{5,4},{6,7},{7,6}} | collective-permute-start | bytes 9437192 | tf_op jit(solution)/shard_map/ppermute | solution.py:340
  706.9 389.6 %collective-permute-start.16 = (bf16[8,512,768]{2,1,0:T(8,128)(2,1)}, bf16[8,512,768]{2,1,0:T(8,128)(2,1)S(1)}, u32[]{:S(2)}, u32[]{:S(2)}) collective-permute-start(bf16[8,512,768]{2,1,0:T(8,128)(2,1)} %get-tuple-element.18.refs_0_), channel_id=1, source_target_pairs={{0,2},{1,3},{2,0},{3,1},{4,6},{5,7},{6,4},{7,5}} | collective-permute-start | bytes 18874376 | tf_op jit(solution)/shard_map/ppermute | solution.py:338
  708.5 391.1 %collective-permute-start.13 = (bf16[8,512,768]{2,1,0:T(8,128)(2,1)}, bf16[8,512,768]{2,1,0:T(8,128)(2,1)S(1)}, u32[]{:S(2)}, u32[]{:S(2)}) collective-permute-start(bf16[8,512,768]{2,1,0:T(8,128)(2,1)} %get-tuple-element.17.refs_0_), channel_id=1, source_target_pairs={{0,2},{1,3},{2,0},{3,1},{4,6},{5,7},{6,4},{7,5}} | collective-permute-start | bytes 18874376 | tf_op jit(solution)/shard_map/ppermute | solution.py:338
  708.9 390.7 %copy-start.12 = (bf16[2,512,768]{2,1,0:T(8,128)(2,1)}, bf16[2,512,768]{2,1,0:T(8,128)(2,1)S(1)}, u32[]{:S(2)}) copy-start(bf16[2,512,768]{2,1,0:T(8,128)(2,1)S(1)} %collective-permute-done.6.refs_1_) | copy-start | bytes 4718596
  708.9 387.6 %collective-permute-start.19 = (bf16[7,512,768]{2,1,0:T(8,128)(2,1)}, bf16[7,512,768]{2,1,0:T(8,128)(2,1)S(1)}, u32[]{:S(2)}, u32[]{:S(2)}) collective-permute-start(bf16[7,512,768]{2,1,0:T(8,128)(2,1)} %get-tuple-element.19.refs_0_), channel_id=1, source_target_pairs={{0,2},{1,3},{2,0},{3,1},{4,6},{5,7},{6,4},{7,5}} | collective-permute-start | bytes 16515080 | tf_op jit(solution)/shard_map/ppermute | solution.py:338
  710.6 427.3 %copy-start.9 = (bf16[4,512,768]{2,1,0:T(8,128)(2,1)}, bf16[4,512,768]{2,1,0:T(8,128)(2,1)S(1)}, u32[]{:S(2)}) copy-start(bf16[4,512,768]{2,1,0:T(8,128)(2,1)S(1)} %collective-permute-done.10.refs_2_) | copy-start | bytes 9437188
  710.6 389.1 %collective-permute-start.18 = (bf16[7,512,768]{2,1,0:T(8,128)(2,1)}, bf16[7,512,768]{2,1,0:T(8,128)(2,1)S(1)}, u32[]{:S(2)}, u32[]{:S(2)}) collective-permute-start(bf16[7,512,768]{2,1,0:T(8,128)(2,1)} %get-tuple-element.19.refs_0_), channel_id=1, source_target_pairs={{0,1},{1,0},{2,3},{3,2},{4,5},{5,4},{6,7},{7,6}} | collective-permute-start | bytes 16515080 | tf_op jit(solution)/shard_map/ppermute | solution.py:340
  710.6 389.1 %copy-start.10 = (bf16[4,512,768]{2,1,0:T(8,128)(2,1)}, bf16[4,512,768]{2,1,0:T(8,128)(2,1)S(1)}, u32[]{:S(2)}) copy-start(bf16[4,512,768]{2,1,0:T(8,128)(2,1)S(1)} %collective-permute-done.9.refs_1_) | copy-start | bytes 9437188
  710.6 389.6 %collective-permute-start.15 = (bf16[8,512,768]{2,1,0:T(8,128)(2,1)}, bf16[8,512,768]{2,1,0:T(8,128)(2,1)S(1)}, u32[]{:S(2)}, u32[]{:S(2)}) collective-permute-start(bf16[8,512,768]{2,1,0:T(8,128)(2,1)} %get-tuple-element.18.refs_0_), channel_id=1, source_target_pairs={{0,1},{1,0},{2,3},{3,2},{4,5},{5,4},{6,7},{7,6}} | collective-permute-start | bytes 18874376 | tf_op jit(solution)/shard_map/ppermute | solution.py:340
  1096.5 41.4 %copy-start.6 = (bf16[7,512,768]{2,1,0:T(8,128)(2,1)}, bf16[7,512,768]{2,1,0:T(8,128)(2,1)S(1)}, u32[]{:S(2)}) copy-start(bf16[7,512,768]{2,1,0:T(8,128)(2,1)S(1)} %collective-permute-done.19.refs_2_) | copy-start | bytes 16515076
  1096.5 10.4 collective-permute-start.12
  1096.5 2.6 copy-start
  1099.2 38.6 %collective-permute-start.17 = (bf16[8,512,768]{2,1,0:T(8,128)(2,1)S(1)}, bf16[8,512,768]{2,1,0:T(8,128)(2,1)S(1)}, u32[]{:S(2)}, u32[]{:S(2)}) collective-permute-start(bf16[8,512,768]{2,1,0:T(8,128)(2,1)S(1)} %collective-permute-done.16.refs_2_), channel_id=1, source_target_pairs={{0,1},{1,0},{2,3},{3,2},{4,5},{5,4},{6,7},{7,6}} | collective-permute-start | bytes 18874376 | tf_op jit(solution)/shard_map/ppermute | solution.py:341
  1099.6 38.1 %copy-start.1 = (bf16[8,512,768]{2,1,0:T(8,128)(2,1)}, bf16[8,512,768]{2,1,0:T(8,128)(2,1)S(1)}, u32[]{:S(2)}) copy-start(bf16[8,512,768]{2,1,0:T(8,128)(2,1)S(1)} %collective-permute-done.13.refs_2_) | copy-start | bytes 18874372
  1099.6 38.3 %collective-permute-start.14 = (bf16[8,512,768]{2,1,0:T(8,128)(2,1)S(1)}, bf16[8,512,768]{2,1,0:T(8,128)(2,1)S(1)}, u32[]{:S(2)}, u32[]{:S(2)}) collective-permute-start(bf16[8,512,768]{2,1,0:T(8,128)(2,1)S(1)} %collective-permute-done.13.refs_2_), channel_id=1, source_target_pairs={{0,1},{1,0},{2,3},{3,2},{4,5},{5,4},{6,7},{7,6}} | collective-permute-start | bytes 18874376 | tf_op jit(solution)/shard_map/ppermute | solution.py:341
  1099.7 38.2 %copy-start.7 = (bf16[7,512,768]{2,1,0:T(8,128)(2,1)}, bf16[7,512,768]{2,1,0:T(8,128)(2,1)S(1)}, u32[]{:S(2)}) copy-start(bf16[7,512,768]{2,1,0:T(8,128)(2,1)S(1)} %collective-permute-done.18.refs_1_) | copy-start | bytes 16515076
  1099.7 37.7 %collective-permute-start.20 = (bf16[7,512,768]{2,1,0:T(8,128)(2,1)S(1)}, bf16[7,512,768]{2,1,0:T(8,128)(2,1)S(1)}, u32[]{:S(2)}, u32[]{:S(2)}) collective-permute-start(bf16[7,512,768]{2,1,0:T(8,128)(2,1)S(1)} %collective-permute-done.19.refs_2_), channel_id=1, source_target_pairs={{0,1},{1,0},{2,3},{3,2},{4,5},{5,4},{6,7},{7,6}} | collective-permute-start | bytes 16515080 | tf_op jit(solution)/shard_map/ppermute | solution.py:341
  1100.2 37.7 %copy-start.2 = (bf16[8,512,768]{2,1,0:T(8,128)(2,1)}, bf16[8,512,768]{2,1,0:T(8,128)(2,1)S(1)}, u32[]{:S(2)}) copy-start(bf16[8,512,768]{2,1,0:T(8,128)(2,1)S(1)} %collective-permute-done.15.refs_1_) | copy-start | bytes 18874372
  1100.2 37.0 %collective-permute-start.11 = (bf16[4,512,768]{2,1,0:T(8,128)(2,1)S(1)}, bf16[4,512,768]{2,1,0:T(8,128)(2,1)S(1)}, u32[]{:S(2)}, u32[]{:S(2)}) collective-permute-start(bf16[4,512,768]{2,1,0:T(8,128)(2,1)S(1)} %collective-permute-done.10.refs_2_), channel_id=1, source_target_pairs={{0,1},{1,0},{2,3},{3,2},{4,5},{5,4},{6,7},{7,6}} | collective-permute-start | bytes 9437192 | tf_op jit(solution)/shard_map/ppermute | solution.py:341
  1106.9 31.1 %copy-start.3 = (bf16[8,512,768]{2,1,0:T(8,128)(2,1)}, bf16[8,512,768]{2,1,0:T(8,128)(2,1)S(1)}, u32[]{:S(2)}) copy-start(bf16[8,512,768]{2,1,0:T(8,128)(2,1)S(1)} %collective-permute-done.12.refs_1_) | copy-start | bytes 18874372
  1106.9 149.5 %collective-permute-start.3 = (bf16[1,512,768]{2,1,0:T(8,128)(2,1)}, bf16[1,512,768]{2,1,0:T(8,128)(2,1)}, u32[]{:S(2)}, u32[]{:S(2)}) collective-permute-start(bf16[1,512,768]{2,1,0:T(8,128)(2,1)} %get-tuple-element.14.refs_0_), channel_id=1, source_target_pairs={{0,1},{1,0},{2,3},{3,2},{4,5},{5,4},{6,7},{7,6}} | collective-permute-start | bytes 2359304 | tf_op jit(solution)/shard_map/ppermute | solution.py:340
  1137.2 1.8 copy-start.11
  1137.2 122.1 %collective-permute-start.2 = (bf16[1,512,768]{2,1,0:T(8,128)(2,1)}, bf16[1,512,768]{2,1,0:T(8,128)(2,1)}, u32[]{:S(2)}, u32[]{:S(2)}) collective-permute-start(bf16[1,512,768]{2,1,0:T(8,128)(2,1)} %get-tuple-element.13.refs_0_), channel_id=1, source_target_pairs={{0,1},{1,0},{2,3},{3,2},{4,5},{5,4},{6,7},{7,6}} | collective-permute-start | bytes 2359304 | tf_op jit(solution)/shard_map/ppermute | solution.py:340
  1137.4 3.3 copy-start.8
  1137.4 119.0 %collective-permute-start.5 = (bf16[1,512,768]{2,1,0:T(8,128)(2,1)}, bf16[1,512,768]{2,1,0:T(8,128)(2,1)}, u32[]{:S(2)}, u32[]{:S(2)}) collective-permute-start(bf16[1,512,768]{2,1,0:T(8,128)(2,1)} %collective-permute-done.4.refs_2_), channel_id=1, source_target_pairs={{0,1},{1,0},{2,3},{3,2},{4,5},{5,4},{6,7},{7,6}} | collective-permute-start | bytes 2359304 | tf_op jit(solution)/shard_map/ppermute | solution.py:341
  1137.8 5.0 copy-start.4
  1137.8 124.3 %collective-permute-start.1 = (bf16[1,512,768]{2,1,0:T(8,128)(2,1)}, bf16[1,512,768]{2,1,0:T(8,128)(2,1)}, u32[]{:S(2)}, u32[]{:S(2)}) collective-permute-start(bf16[1,512,768]{2,1,0:T(8,128)(2,1)} %collective-permute-done.refs_2_), channel_id=1, source_target_pairs={{0,1},{1,0},{2,3},{3,2},{4,5},{5,4},{6,7},{7,6}} | collective-permute-start | bytes 2359304 | tf_op jit(solution)/shard_map/ppermute | solution.py:341
  1142.7 2.7 copy-start.5
  1145.4 105.5 %collective-permute-start.8 = (bf16[2,512,768]{2,1,0:T(8,128)(2,1)}, bf16[2,512,768]{2,1,0:T(8,128)(2,1)}, u32[]{:S(2)}, u32[]{:S(2)}) collective-permute-start(bf16[2,512,768]{2,1,0:T(8,128)(2,1)} %collective-permute-done.7.refs_2_), channel_id=1, source_target_pairs={{0,1},{1,0},{2,3},{3,2},{4,5},{5,4},{6,7},{7,6}} | collective-permute-start | bytes 4718600 | tf_op jit(solution)/shard_map/ppermute | solution.py:341

commit v2 on v1

--- a/solution.py
+++ b/solution.py
@@ -19,8 +19,9 @@
 COEF_C = 2.0315
 
 GROUP = 4
-CHUNKS = (1, 7, 8, 8, 4, 2, 1, 1)
+CHUNKS = (2, 6, 8, 8, 4, 2, 1, 1)
 FIRSTS = tuple(sum(CHUNKS[:c]) for c in range(len(CHUNKS)))
+PIECES = 4
 ORDER = (2, 3, 1, 0)
 X_PERM = ((0, 2), (1, 3), (2, 0), (3, 1))
 CORE_PERM = ((0, 1), (1, 0), (2, 3), (3, 2))
@@ -35,7 +36,8 @@
     n = len(CHUNKS)
     w_outs, (w_chip, mb, xin, oo, orv) = refs[:n], refs[n : n + 5]
     (fbuf, hbuf, sbuf, ss_loc, ss_in, xa, xb, amat, bmat, f_sem, h_sem, st_sem, x_sem,
-     m_send, m_recv, s_send, s_recv, o_send, o_recv, w_send, w_recv) = refs[n + 5 :]
+     m_send, m_recv, s_send, s_recv, o_send, o_recv, w_send, w_recv, turn,
+     pf_sem, ph_sem, ps_sem) = refs[n + 5 :]
     rows, cols = mom_ref.shape[1], mom_ref.shape[2]
     rel = relations(lax.axis_index("data"))
     strip = 64
@@ -43,7 +45,6 @@
     barrier = pltpu.get_barrier_semaphore()
     for k in (1, 2, 3):
         pl.semaphore_signal(barrier, inc=1, device_id={"data": rel[k]}, device_id_type=pl.DeviceIdType.MESH)
-    pl.semaphore_wait(barrier, GROUP - 1)
 
     def remote(src, dst, send, recv, k):
         return pltpu.make_async_remote_copy(
@@ -59,53 +60,108 @@
         dst = xin.at[r, pl.ds(0, rows)] if k == 0 else mb.at[r, k - 1]
         return pltpu.make_async_copy(sbuf.at[slot], dst, st_sem.at[slot])
 
+    def send_sum(r, k):
+        return remote(ss_loc.at[r, k - 1], ss_in.at[r, k], s_send.at[r, k - 1], s_recv.at[r, k - 1], k)
+
     def send_m(r, k):
         return (remote(mb.at[r, k - 1], xin.at[r, pl.ds(k * rows, rows)], m_send.at[r, k - 1], m_recv.at[r, k - 1], k),
-                remote(ss_loc.at[r, k - 1], ss_in.at[r, k], s_send.at[r, k - 1], s_recv.at[r, k - 1], k))
-
-    for copy in load_m(0, ORDER[0], 0):
+                send_sum(r, k))
+
+    def block_m(r, j):
+        k, slot = ORDER[j], j % 2
+        for copy in load_m(r, k, slot):
+            copy.wait()
+        if j + 1 < GROUP:
+            for copy in load_m(r, ORDER[j + 1], 1 - slot):
+                copy.start()
+        else:
+            @pl.when(r + 1 < rounds)
+            def _():
+                for copy in load_m(r + 1, ORDER[0], 1 - slot):
+                    copy.start()
+
+        keep_sum(r, k, lax.fori_loop(0, rows // strip, momentum_strip(slot), jnp.zeros((8, cols), jnp.float32)))
+        stage_m(r, k, slot).start()
+
+    def momentum_strip(slot):
+        def part(i, acc):
+            sl = pl.ds(pl.multiple_of(i * strip, strip), strip)
+            mom_new = MOMENTUM * fbuf[slot, sl, :] + hbuf[slot, sl, :].astype(jnp.float32)
+            sbuf[slot, sl, :] = mom_new.astype(jnp.bfloat16)
+            return acc + jnp.sum((mom_new * mom_new).reshape(strip // 8, 8, cols), axis=0)
+
+        return part
+
+    def keep_sum(r, k, acc):
+        total = jnp.broadcast_to(jnp.sum(jnp.sum(acc, axis=0, keepdims=True), axis=1, keepdims=True), (8, 128))
+        if k == 0:
+            ss_in[r, 0] = total
+        else:
+            ss_loc[r, k - 1] = total
+
+    def staged_m(r, j):
+        stage_m(r, ORDER[j], j % 2).wait()
+        if ORDER[j] != 0:
+            for copy in send_m(r, ORDER[j]):
+                copy.start()
+
+    first, height = ORDER[0], rows // PIECES
+    pieces = [pl.ds(n * height, height) for n in range(PIECES)]
+
+    def load_piece(n):
+        m = rel[first]
+        return (pltpu.make_async_copy(mom_ref.at[m, pieces[n]], fbuf.at[0, pieces[n]], pf_sem.at[n]),
+                pltpu.make_async_copy(grad_ref.at[m, pieces[n]], hbuf.at[0, pieces[n]], ph_sem.at[n]))
+
+    def stage_piece(n):
+        return pltpu.make_async_copy(sbuf.at[0, pieces[n]], mb.at[0, first - 1, pieces[n]], ps_sem.at[n])
+
+    def send_piece(n):
+        stage_piece(n).wait()
+        remote(mb.at[0, first - 1, pieces[n]], xin.at[0, pl.ds(first * rows + n * height, height)],
+               m_send.at[0, first - 1], m_recv.at[0, first - 1], first).start()
+
+    for p in range(PIECES):
+        for copy in load_piece(p):
+            copy.start()
+    for copy in load_m(0, ORDER[1], 1):
         copy.start()
+    acc = jnp.zeros((8, cols), jnp.float32)
+    for p in range(PIECES):
+        for copy in load_piece(p):
+            copy.wait()
+        acc = lax.fori_loop(p * height // strip, (p + 1) * height // strip, momentum_strip(0), acc)
+        stage_piece(p).start()
+        if p == 0:
+            pl.semaphore_wait(barrier, GROUP - 1)
+        else:
+            send_piece(p - 1)
+    keep_sum(0, first, acc)
+    send_piece(PIECES - 1)
 
     def momentum_round(r, carry):
-        for j, k in enumerate(ORDER):
-            slot = j % 2
-            for copy in load_m(r, k, slot):
-                copy.wait()
-            if j + 1 < GROUP:
-                for copy in load_m(r, ORDER[j + 1], 1 - slot):
-                    copy.start()
-            else:
-                @pl.when(r + 1 < rounds)
-                def _():
-                    for copy in load_m(r + 1, ORDER[0], 1 - slot):
-                        copy.start()
-
-            def part(i, acc):
-                sl = pl.ds(pl.multiple_of(i * strip, strip), strip)
-                mom_new = MOMENTUM * fbuf[slot, sl, :] + hbuf[slot, sl, :].astype(jnp.float32)
-                sbuf[slot, sl, :] = mom_new.astype(jnp.bfloat16)
-                return acc + jnp.sum((mom_new * mom_new).reshape(strip // 8, 8, cols), axis=0)
-
-            acc = lax.fori_loop(0, rows // strip, part, jnp.zeros((8, cols), jnp.float32))
-            total = jnp.broadcast_to(jnp.sum(jnp.sum(acc, axis=0, keepdims=True), axis=1, keepdims=True), (8, 128))
-            if k == 0:
-                ss_in[r, 0] = total
-            else:
-                ss_loc[r, k - 1] = total
-            stage_m(r, k, slot).start()
-            if j > 0:
-                before = ORDER[j - 1]
-                stage_m(r, before, 1 - slot).wait()
-                for copy in send_m(r, before):
-                    copy.start()
-            else:
-                @pl.when(r > 0)
-                def _():
-                    stage_m(r - 1, ORDER[-1], 1 - slot).wait()
+        @pl.when(r > 0)
+        def _():
+            block_m(r, 0)
+            staged_m(r - 1, GROUP - 1)
+
+        block_m(r, 1)
+
+        @pl.when(r > 0)
+        def _():
+            staged_m(r, 0)
+
+        @pl.when(r == 0)
+        def _():
+            send_sum(r, first).start()
+
+        for j in range(2, GROUP):
+            block_m(r, j)
+            staged_m(r, j - 1)
         return carry
 
     lax.fori_loop(0, rounds, momentum_round, 0)
-    stage_m(rounds - 1, ORDER[-1], (GROUP - 1) % 2).wait()
+    staged_m(rounds - 1, GROUP - 1)
 
     def send_o(r, k):
         return remote(oo.at[r, pl.ds(k * rows, rows)], orv.at[r, rel[0]], o_send.at[r, k - 1], o_recv.at[r, k - 1], k)
@@ -190,7 +246,7 @@
         def _():
             stage_w(0, 0, slot).wait()
 
-        @pl.when(m == CHUNKS[0] + 1)
+        @pl.when((m == CHUNKS[0] + 1) & (lax.rem(rel[0], 2) == 0))
         def _():
             for i in range(CHUNKS[0]):
                 send_w(i).start()
@@ -203,7 +259,7 @@
             return c
 
         lax.fori_loop(0, rows // strip, part, 0)
-        for c in range(n):
+        for c in range(len(CHUNKS)):
             @pl.when((m >= FIRSTS[c]) & (m < FIRSTS[c] + CHUNKS[c]))
             def _():
                 stage_w(c, m - FIRSTS[c], slot).start()
@@ -217,8 +273,24 @@
     lax.fori_loop(0, mats, weights, 0)
     stage_w(0, 0, 0).wait()
     stage_w(0, 0, 1).wait()
+
+    @pl.when(lax.rem(rel[0], 2) == 0)
+    def _():
+        send_w(0).wait_send()
+        pl.semaphore_signal(turn, inc=1, device_id={"data": rel[1]}, device_id_type=pl.DeviceIdType.MESH)
+        for i in range(1, CHUNKS[0]):
+            send_w(i).wait_send()
+
+    @pl.when(lax.rem(rel[0], 2) == 1)
+    def _():
+        pl.semaphore_wait(turn, 1)
+        for i in range(CHUNKS[0]):
+            send_w(i).start()
+        for i in range(CHUNKS[0]):
+            send_w(i).wait_send()
+
     for i in range(CHUNKS[0]):
-        send_w(i).wait()
+        send_w(i).wait_recv()
 
     def drain(r, carry):
         for k in (1, 2, 3):
@@ -259,7 +331,8 @@
             pltpu.VMEM((cols, cols), half),
             pltpu.VMEM((cols, cols), half),
             dma((2,)), dma((2,)), dma((2,)), dma,
-            *[dma((rounds, 3))] * 6, *[dma((CHUNKS[0],))] * 2,
+            *[dma((rounds, 3))] * 6, *[dma((CHUNKS[0],))] * 2, pltpu.SemaphoreType.REGULAR,
+            *[dma((PIECES,))] * 3,
         ],
         compiler_params=pltpu.CompilerParams(collective_id=0, has_side_effects=True, vmem_limit_bytes=60 * 1024 * 1024),
         cost_estimate=pl.CostEstimate(flops=flops, bytes_accessed=12 * mats * rows * cols, transcendentals=0),
@@ -320,6 +393,7 @@
         out_specs=pl.BlockSpec(memory_space=pltpu.HBM),
         scratch_shapes=[pltpu.VMEM((2, len(parts), rows, cols), jnp.bfloat16), dma((2, len(parts))), dma((2, len(parts)))],
         input_output_aliases=aliases,
+        compiler_params=pltpu.CompilerParams(vmem_limit_bytes=67_043_328),
         cost_estimate=pl.CostEstimate(flops=size, bytes_accessed=4 * size, transcendentals=0),
         name="place",
     )(*args)
@@ -344,7 +418,8 @@
         params = None
         for c in range(last):
             params = place(c, {0: own[c], 1: core[c], 2: chip[c], 3: diag[c]}, params, mats)
-        params = place(last, {0: own[last], 1: core[last], 2: chip[last]}, params, mats)
+        params = place(last, {0: own[last], 1: core[last]}, params, mats)
+        params = place(last, {2: chip[last]}, params, mats)
         params = place(last, {3: diag[last]}, params, mats)
         return params, mom_new
 

time: 1270 us -> 1260 us (level)
  waiting for transfers between devices: 555 us -> 524 us
  starting transfers between devices: 11.4 us -> 31.6 us
    ppermute x7, waiting for transfers between devices: 518 us -> 488 us  [local_step(): chip.append(lax.ppermute(own[c], 'data', X_PERM))]
    ppermute x8, starting transfers between devices: 0.8 us -> 23.5 us  [local_step(): core.append(lax.ppermute(own[c], 'data', CORE_PERM))]
    pallas_call x9 -> x10, Pallas kernels: 77 us -> 79.7 us  [place(): pl.pallas_call(functools.partial(place_kernel, FIRSTS[chunk], parts), out...]
  transfers between devices with their start and end apart: 23 -> 23, of which waited for: 5 -> 4; matrix products, arithmetic and copies ran while one was open for 3% -> 3% of each run, Pallas kernels for 6% -> 6%
where the time goes in v2:
time: 1260 us
  Pallas kernels  652 us (52%)
  waiting for transfers between devices  524 us (42%)
  other arithmetic  41.4 us (3%)
  starting transfers between devices  31.6 us (3%)
    pallas_call x1, Pallas kernels, exchange(): pl.pallas_call(functools.partial(exchange_kernel, rounds, rms_scale), out...  572 us
    ppermute x7, waiting for transfers between devices, local_step(): chip.append(lax.ppermute(own[c], 'data', X_PERM))  488 us
    pallas_call x10, Pallas kernels, place(): pl.pallas_call(functools.partial(place_kernel, FIRSTS[chunk], parts), out...  79.7 us
    add x1, other arithmetic, local_step(): mom_new = MOMENTUM * mom_late + grad_late.astype(jnp.float32)  41.4 us
    ppermute x8, waiting for transfers between devices, local_step(): diag.append(lax.ppermute(chip[c], 'data', CORE_PERM))  29.1 us
  transfers between devices with their start and end apart: 23, of which 4 were waited for; matrix products, arithmetic and copies ran while one was open for 3% of the time, Pallas kernels for 6%

profile of v2, /device:TPU:0, one launch (start us, length us, event | category | flops | bytes accessed | tf_op | source)
XLA Modules:
  0.0 1261.3 jit_solution(12188528833616616775)
XLA Ops:
  0.6 571.9 %exchange.1 = (bf16[2,512,768]{2,1,0:T(8,128)(2,1)}, bf16[6,512,768]{2,1,0:T(8,128)(2,1)}, bf16[8,512,768]{2,1,0:T(8,128)(2,1)}, bf16[8,512,768]{2,1,0:T(8,128)(...) custom-call(f32[32,512,768]{2,1,0:T(8,128)} %w_ref.1, ...), custom_call_target="tpu_custom_call" | custom-call | flops 229512314880 | bytes 150994944 | tf_op jit(solution)/shard_map/exchange/pallas_call | solution.py:318
  572.5 0.0 collective-permute-start.4
  572.6 16.0 %collective-permute-start.21 = (bf16[2,512,768]{2,1,0:T(8,128)(2,1)}, bf16[2,512,768]{2,1,0:T(8,128)(2,1)S(1)}, u32[]{:S(2)}, u32[]{:S(2)}) collective-permute-start(bf16[2,512,768]{2,1,0:T(8,128)(2,1)} %get-tuple-element.20.refs_0_), channel_id=1, source_target_pairs={{0,1},{1,0},{2,3},{3,2},{4,5},{5,4},{6,7},{7,6}} | collective-permute-start | bytes 4718600 | tf_op jit(solution)/shard_map/ppermute | solution.py:414
  588.6 0.0 collective-permute-start.22
  588.6 0.8 collective-permute-start.7
  589.4 1.2 collective-permute-start.10
  590.6 0.0 collective-permute-done.4.refs_2_
  590.6 0.8 collective-permute-start
  591.4 118.9 %collective-permute-done.refs_0_ = bf16[1,512,768]{2,1,0:T(8,128)(2,1)S(1)} collective-permute-done((bf16[1,512,768]{2,1,0:T(8,128)(2,1)}, bf16[1,512,768]{2,1,0:T(8,128)(2,1)S(1)}, u32[]{:S(2)}, u32[]{:S(2)}) %collective-permute-start) | collective-permute-done | bytes 786464 | tf_op jit(solution)/shard_map/ppermute | solution.py:412
  710.3 6.3 collective-permute-start.9
  716.7 0.0 collective-permute-done.21.refs_1_
  716.7 1.1 copy-done.11
  717.8 1.2 collective-permute-start.16
  719.0 0.0 collective-permute-done.22.refs_3_
  719.0 1.1 copy-done.12
  720.2 0.8 collective-permute-start.13
  721.0 0.0 collective-permute-done.7.refs_2_
  721.0 1.2 collective-permute-start.19
  722.2 0.0 collective-permute-done.10.refs_2_
  722.2 0.1 collective-permute-start.15
  722.3 0.0 collective-permute-done.9.refs_1_
  722.3 0.4 collective-permute-start.18
  722.7 369.5 %collective-permute-done.19.refs_2_ = bf16[6,512,768]{2,1,0:T(8,128)(2,1)S(1)} collective-permute-done((bf16[6,512,768]{2,1,0:T(8,128)(2,1)}, bf16[6,512,768]{2,1,0:T(8,128)(2,1)S(1)}, u32[]{:S(2)}, u32[]{:S(2)}) %collective-permute-start.19) | collective-permute-done | bytes 4718624 | tf_op jit(solution)/shard_map/ppermute | solution.py:412
  1092.3 0.0 collective-permute-start.12
  1092.3 0.0 collective-permute-done.16.refs_2_
  1092.3 2.7 copy-done
  1095.0 0.7 collective-permute-start.17
  1095.7 0.0 collective-permute-done.13.refs_2_
  1095.7 0.0 collective-permute-start.14
  1095.7 0.0 collective-permute-done.18.refs_1_
  1095.8 0.5 collective-permute-start.20
  1096.2 0.0 collective-permute-done.15.refs_1_
  1096.2 0.0 collective-permute-start.11
  1096.3 6.4 collective-permute-done.12.refs_1_
  1102.7 0.1 collective-permute-start.6
  1102.8 29.1 %collective-permute-done.11.refs_3_ = bf16[4,512,768]{2,1,0:T(8,128)(2,1)S(1)} collective-permute-done((bf16[4,512,768]{2,1,0:T(8,128)(2,1)S(1)}, bf16[4,512,768]{2,1,0:T(8,128)(2,1)S(1)}, u32[]{:S(2)}, u32[]{:S(2)}) %collective-permute-start.11) | collective-permute-done | bytes 3145760 | tf_op jit(solution)/shard_map/ppermute | solution.py:415
  1131.9 0.1 collective-permute-start.8
  1132.1 0.4 collective-permute-start.3
  1132.4 0.0 collective-permute-done.17.refs_3_
  1132.4 0.2 collective-permute-start.5
  1132.6 0.0 collective-permute-done.14.refs_3_
  1132.6 1.0 copy-done.10
  1133.6 1.3 copy-done.8
  1134.9 2.0 copy-done.4
  1137.0 2.6 copy-done.5
  1139.6 0.1 collective-permute-start.2
  1139.7 5.5 place.10.refs_4_
  1145.2 13.8 %place.11.refs_4_ = bf16[32,2048,768]{2,1,0:T(8,128)(2,1)} custom-call(bf16[6,512,768]{2,1,0:T(8,128)(2,1)} %get-tuple-element.19.refs_0_, bf16[6,512,768]{2,1,0:T(8,128)(2,1)} %copy-done.7, bf16[6,512,768]{2,1,0:T(8,128)(2,1)} %copy-done.6, bf16[6,512,768]{2,1,0:T(8,128)(2,1)} %copy-done.8, ...), custom_call_target="tpu_custom_call", output_to_operand_aliasing={{}: (4, {})} | custom-call | flops 9437184 | bytes 37748736 | tf_op jit(solution)/shard_map/place/pallas_call | solution.py:389
  1159.0 18.0 %place.12.refs_4_ = bf16[32,2048,768]{2,1,0:T(8,128)(2,1)} custom-call(bf16[8,512,768]{2,1,0:T(8,128)(2,1)} %get-tuple-element.18.refs_0_, bf16[8,512,768]{2,1,0:T(8,128)(2,1)} %copy-done.2, bf16[8,512,768]{2,1,0:T(8,128)(2,1)} %copy-done, bf16[8,512,768]{2,1,0:T(8,128)(2,1)} %copy-done.4, ...), custom_call_target="tpu_custom_call", output_to_operand_aliasing={{}: (4, {})} | custom-call | flops 12582912 | bytes 50331648 | tf_op jit(solution)/shard_map/place/pallas_call | solution.py:389
  1177.0 18.0 %place.13.refs_4_ = bf16[32,2048,768]{2,1,0:T(8,128)(2,1)} custom-call(bf16[8,512,768]{2,1,0:T(8,128)(2,1)} %get-tuple-element.17.refs_0_, bf16[8,512,768]{2,1,0:T(8,128)(2,1)} %copy-done.3, bf16[8,512,768]{2,1,0:T(8,128)(2,1)} %copy-done.1, bf16[8,512,768]{2,1,0:T(8,128)(2,1)} %copy-done.5, ...), custom_call_target="tpu_custom_call", output_to_operand_aliasing={{}: (4, {})} | custom-call | flops 12582912 | bytes 50331648 | tf_op jit(solution)/shard_map/place/pallas_call | solution.py:389
  1194.9 9.6 place.14.refs_4_
  1204.6 0.0 collective-permute-done.6.refs_1_
  1204.6 0.4 collective-permute-start.1
  1205.0 0.0 collective-permute-done.8.refs_3_
  1205.0 5.5 place.15.refs_4_
  1210.5 0.0 collective-permute-done.3.refs_1_
  1210.5 0.0 collective-permute-done.5.refs_3_
  1210.5 2.9 place.16.refs_2_
  1213.4 0.0 collective-permute-done.2.refs_1_
  1213.4 2.3 place.17.refs_1_
  1215.8 41.4 %convert_add_fusion = f32[32,512,768]{2,1,0:T(8,128)} fusion(bf16[32,512,768]{2,1,0:T(8,128)(2,1)} %grad_ref.1, f32[32,512,768]{2,1,0:T(8,128)} %mom_ref.1), kind=kLoop, calls=%fused_computation | loop fusion | flops 37748736 | bytes 125829120 | tf_op jit(solution)/shard_map/add | solution.py:417
  1257.2 2.0 place.18.refs_1_
  1259.2 0.0 collective-permute-done.1.refs_0_
  1259.2 2.1 place.19
  (22 shorter events, 0.0 us)
Async XLA Ops:
  572.5 18.1 %collective-permute-start.4 = (bf16[1,512,768]{2,1,0:T(8,128)(2,1)}, bf16[1,512,768]{2,1,0:T(8,128)(2,1)}, u32[]{:S(2)}, u32[]{:S(2)}) collective-permute-start(bf16[1,512,768]{2,1,0:T(8,128)(2,1)} %get-tuple-element.14.refs_0_), channel_id=1, source_target_pairs={{0,2},{1,3},{2,0},{3,1},{4,6},{5,7},{6,4},{7,5}} | collective-permute-start | bytes 2359304 | tf_op jit(solution)/shard_map/ppermute | solution.py:412
  572.6 144.1 %collective-permute-start.21 = (bf16[2,512,768]{2,1,0:T(8,128)(2,1)}, bf16[2,512,768]{2,1,0:T(8,128)(2,1)S(1)}, u32[]{:S(2)}, u32[]{:S(2)}) collective-permute-start(bf16[2,512,768]{2,1,0:T(8,128)(2,1)} %get-tuple-element.20.refs_0_), channel_id=1, source_target_pairs={{0,1},{1,0},{2,3},{3,2},{4,5},{5,4},{6,7},{7,6}} | collective-permute-start | bytes 4718600 | tf_op jit(solution)/shard_map/ppermute | solution.py:414
  588.6 130.5 %collective-permute-start.22 = (bf16[2,512,768]{2,1,0:T(8,128)(2,1)}, bf16[2,512,768]{2,1,0:T(8,128)(2,1)S(1)}, u32[]{:S(2)}, u32[]{:S(2)}) collective-permute-start(bf16[2,512,768]{2,1,0:T(8,128)(2,1)} %get-tuple-element.21.refs_2_), channel_id=1, source_target_pairs={{0,1},{1,0},{2,3},{3,2},{4,5},{5,4},{6,7},{7,6}} | collective-permute-start | bytes 4718600 | tf_op jit(solution)/shard_map/ppermute | solution.py:415
  588.6 132.4 %collective-permute-start.7 = (bf16[2,512,768]{2,1,0:T(8,128)(2,1)}, bf16[2,512,768]{2,1,0:T(8,128)(2,1)}, u32[]{:S(2)}, u32[]{:S(2)}) collective-permute-start(bf16[2,512,768]{2,1,0:T(8,128)(2,1)} %get-tuple-element.15.refs_0_), channel_id=1, source_target_pairs={{0,2},{1,3},{2,0},{3,1},{4,6},{5,7},{6,4},{7,5}} | collective-permute-start | bytes 4718600 | tf_op jit(solution)/shard_map/ppermute | solution.py:412
  589.4 132.8 %collective-permute-start.10 = (bf16[4,512,768]{2,1,0:T(8,128)(2,1)}, bf16[4,512,768]{2,1,0:T(8,128)(2,1)S(1)}, u32[]{:S(2)}, u32[]{:S(2)}) collective-permute-start(bf16[4,512,768]{2,1,0:T(8,128)(2,1)} %get-tuple-element.16.refs_0_), channel_id=1, source_target_pairs={{0,2},{1,3},{2,0},{3,1},{4,6},{5,7},{6,4},{7,5}} | collective-permute-start | bytes 9437192 | tf_op jit(solution)/shard_map/ppermute | solution.py:412
  590.6 119.7 %collective-permute-start = (bf16[1,512,768]{2,1,0:T(8,128)(2,1)}, bf16[1,512,768]{2,1,0:T(8,128)(2,1)S(1)}, u32[]{:S(2)}, u32[]{:S(2)}) collective-permute-start(bf16[1,512,768]{2,1,0:T(8,128)(2,1)} %get-tuple-element.13.refs_0_), channel_id=1, source_target_pairs={{0,2},{1,3},{2,0},{3,1},{4,6},{5,7},{6,4},{7,5}} | collective-permute-start | bytes 2359304 | tf_op jit(solution)/shard_map/ppermute | solution.py:412
  710.3 6.4 copy-start.13
  710.3 12.0 collective-permute-start.9
  716.7 1.1 copy-start.11
  717.8 374.5 %collective-permute-start.16 = (bf16[8,512,768]{2,1,0:T(8,128)(2,1)}, bf16[8,512,768]{2,1,0:T(8,128)(2,1)S(1)}, u32[]{:S(2)}, u32[]{:S(2)}) collective-permute-start(bf16[8,512,768]{2,1,0:T(8,128)(2,1)} %get-tuple-element.18.refs_0_), channel_id=1, source_target_pairs={{0,2},{1,3},{2,0},{3,1},{4,6},{5,7},{6,4},{7,5}} | collective-permute-start | bytes 18874376 | tf_op jit(solution)/shard_map/ppermute | solution.py:412
  719.0 1.2 copy-start.12
  720.2 375.5 %collective-permute-start.13 = (bf16[8,512,768]{2,1,0:T(8,128)(2,1)}, bf16[8,512,768]{2,1,0:T(8,128)(2,1)S(1)}, u32[]{:S(2)}, u32[]{:S(2)}) collective-permute-start(bf16[8,512,768]{2,1,0:T(8,128)(2,1)} %get-tuple-element.17.refs_0_), channel_id=1, source_target_pairs={{0,2},{1,3},{2,0},{3,1},{4,6},{5,7},{6,4},{7,5}} | collective-permute-start | bytes 18874376 | tf_op jit(solution)/shard_map/ppermute | solution.py:412
  721.0 371.3 %collective-permute-start.19 = (bf16[6,512,768]{2,1,0:T(8,128)(2,1)}, bf16[6,512,768]{2,1,0:T(8,128)(2,1)S(1)}, u32[]{:S(2)}, u32[]{:S(2)}) collective-permute-start(bf16[6,512,768]{2,1,0:T(8,128)(2,1)} %get-tuple-element.19.refs_0_), channel_id=1, source_target_pairs={{0,2},{1,3},{2,0},{3,1},{4,6},{5,7},{6,4},{7,5}} | collective-permute-start | bytes 14155784 | tf_op jit(solution)/shard_map/ppermute | solution.py:412
  722.2 410.4 %copy-start.9 = (bf16[4,512,768]{2,1,0:T(8,128)(2,1)}, bf16[4,512,768]{2,1,0:T(8,128)(2,1)S(1)}, u32[]{:S(2)}) copy-start(bf16[4,512,768]{2,1,0:T(8,128)(2,1)S(1)} %collective-permute-done.10.refs_2_) | copy-start | bytes 9437188
  722.2 374.0 %collective-permute-start.15 = (bf16[8,512,768]{2,1,0:T(8,128)(2,1)}, bf16[8,512,768]{2,1,0:T(8,128)(2,1)S(1)}, u32[]{:S(2)}, u32[]{:S(2)}) collective-permute-start(bf16[8,512,768]{2,1,0:T(8,128)(2,1)} %get-tuple-element.18.refs_0_), channel_id=1, source_target_pairs={{0,1},{1,0},{2,3},{3,2},{4,5},{5,4},{6,7},{7,6}} | collective-permute-start | bytes 18874376 | tf_op jit(solution)/shard_map/ppermute | solution.py:414
  722.3 373.4 %collective-permute-start.18 = (bf16[6,512,768]{2,1,0:T(8,128)(2,1)}, bf16[6,512,768]{2,1,0:T(8,128)(2,1)S(1)}, u32[]{:S(2)}, u32[]{:S(2)}) collective-permute-start(bf16[6,512,768]{2,1,0:T(8,128)(2,1)} %get-tuple-element.19.refs_0_), channel_id=1, source_target_pairs={{0,1},{1,0},{2,3},{3,2},{4,5},{5,4},{6,7},{7,6}} | collective-permute-start | bytes 14155784 | tf_op jit(solution)/shard_map/ppermute | solution.py:414
  1092.3 40.3 %copy-start.6 = (bf16[6,512,768]{2,1,0:T(8,128)(2,1)}, bf16[6,512,768]{2,1,0:T(8,128)(2,1)S(1)}, u32[]{:S(2)}) copy-start(bf16[6,512,768]{2,1,0:T(8,128)(2,1)S(1)} %collective-permute-done.19.refs_2_) | copy-start | bytes 14155780
  1092.3 10.4 collective-permute-start.12
  1092.3 2.7 copy-start
  1095.0 37.4 %collective-permute-start.17 = (bf16[8,512,768]{2,1,0:T(8,128)(2,1)S(1)}, bf16[8,512,768]{2,1,0:T(8,128)(2,1)S(1)}, u32[]{:S(2)}, u32[]{:S(2)}) collective-permute-start(bf16[8,512,768]{2,1,0:T(8,128)(2,1)S(1)} %collective-permute-done.16.refs_2_), channel_id=1, source_target_pairs={{0,1},{1,0},{2,3},{3,2},{4,5},{5,4},{6,7},{7,6}} | collective-permute-start | bytes 18874376 | tf_op jit(solution)/shard_map/ppermute | solution.py:415
  1095.7 36.7 %copy-start.1 = (bf16[8,512,768]{2,1,0:T(8,128)(2,1)}, bf16[8,512,768]{2,1,0:T(8,128)(2,1)S(1)}, u32[]{:S(2)}) copy-start(bf16[8,512,768]{2,1,0:T(8,128)(2,1)S(1)} %collective-permute-done.13.refs_2_) | copy-start | bytes 18874372
  1095.7 36.9 %collective-permute-start.14 = (bf16[8,512,768]{2,1,0:T(8,128)(2,1)S(1)}, bf16[8,512,768]{2,1,0:T(8,128)(2,1)S(1)}, u32[]{:S(2)}, u32[]{:S(2)}) collective-permute-start(bf16[8,512,768]{2,1,0:T(8,128)(2,1)S(1)} %collective-permute-done.13.refs_2_), channel_id=1, source_target_pairs={{0,1},{1,0},{2,3},{3,2},{4,5},{5,4},{6,7},{7,6}} | collective-permute-start | bytes 18874376 | tf_op jit(solution)/shard_map/ppermute | solution.py:415
  1095.8 36.9 %copy-start.7 = (bf16[6,512,768]{2,1,0:T(8,128)(2,1)}, bf16[6,512,768]{2,1,0:T(8,128)(2,1)S(1)}, u32[]{:S(2)}) copy-start(bf16[6,512,768]{2,1,0:T(8,128)(2,1)S(1)} %collective-permute-done.18.refs_1_) | copy-start | bytes 14155780
  1095.8 36.3 %collective-permute-start.20 = (bf16[6,512,768]{2,1,0:T(8,128)(2,1)S(1)}, bf16[6,512,768]{2,1,0:T(8,128)(2,1)S(1)}, u32[]{:S(2)}, u32[]{:S(2)}) collective-permute-start(bf16[6,512,768]{2,1,0:T(8,128)(2,1)S(1)} %collective-permute-done.19.refs_2_), channel_id=1, source_target_pairs={{0,1},{1,0},{2,3},{3,2},{4,5},{5,4},{6,7},{7,6}} | collective-permute-start | bytes 14155784 | tf_op jit(solution)/shard_map/ppermute | solution.py:415
  1096.2 36.4 %copy-start.2 = (bf16[8,512,768]{2,1,0:T(8,128)(2,1)}, bf16[8,512,768]{2,1,0:T(8,128)(2,1)S(1)}, u32[]{:S(2)}) copy-start(bf16[8,512,768]{2,1,0:T(8,128)(2,1)S(1)} %collective-permute-done.15.refs_1_) | copy-start | bytes 18874372
  1096.2 35.7 %collective-permute-start.11 = (bf16[4,512,768]{2,1,0:T(8,128)(2,1)S(1)}, bf16[4,512,768]{2,1,0:T(8,128)(2,1)S(1)}, u32[]{:S(2)}, u32[]{:S(2)}) collective-permute-start(bf16[4,512,768]{2,1,0:T(8,128)(2,1)S(1)} %collective-permute-done.10.refs_2_), channel_id=1, source_target_pairs={{0,1},{1,0},{2,3},{3,2},{4,5},{5,4},{6,7},{7,6}} | collective-permute-start | bytes 9437192 | tf_op jit(solution)/shard_map/ppermute | solution.py:415
  1102.7 30.0 %copy-start.3 = (bf16[8,512,768]{2,1,0:T(8,128)(2,1)}, bf16[8,512,768]{2,1,0:T(8,128)(2,1)S(1)}, u32[]{:S(2)}) copy-start(bf16[8,512,768]{2,1,0:T(8,128)(2,1)S(1)} %collective-permute-done.12.refs_1_) | copy-start | bytes 18874372
  1102.7 101.9 %collective-permute-start.6 = (bf16[2,512,768]{2,1,0:T(8,128)(2,1)}, bf16[2,512,768]{2,1,0:T(8,128)(2,1)}, u32[]{:S(2)}, u32[]{:S(2)}) collective-permute-start(bf16[2,512,768]{2,1,0:T(8,128)(2,1)} %get-tuple-element.15.refs_0_), channel_id=1, source_target_pairs={{0,1},{1,0},{2,3},{3,2},{4,5},{5,4},{6,7},{7,6}} | collective-permute-start | bytes 4718600 | tf_op jit(solution)/shard_map/ppermute | solution.py:414
  1131.9 1.7 copy-start.10
  1131.9 73.1 %collective-permute-start.8 = (bf16[2,512,768]{2,1,0:T(8,128)(2,1)}, bf16[2,512,768]{2,1,0:T(8,128)(2,1)}, u32[]{:S(2)}, u32[]{:S(2)}) collective-permute-start(bf16[2,512,768]{2,1,0:T(8,128)(2,1)} %collective-permute-done.7.refs_2_), channel_id=1, source_target_pairs={{0,1},{1,0},{2,3},{3,2},{4,5},{5,4},{6,7},{7,6}} | collective-permute-start | bytes 4718600 | tf_op jit(solution)/shard_map/ppermute | solution.py:415
  1132.1 2.9 copy-start.8
  1132.1 78.4 %collective-permute-start.3 = (bf16[1,512,768]{2,1,0:T(8,128)(2,1)}, bf16[1,512,768]{2,1,0:T(8,128)(2,1)}, u32[]{:S(2)}, u32[]{:S(2)}) collective-permute-start(bf16[1,512,768]{2,1,0:T(8,128)(2,1)} %get-tuple-element.14.refs_0_), channel_id=1, source_target_pairs={{0,1},{1,0},{2,3},{3,2},{4,5},{5,4},{6,7},{7,6}} | collective-permute-start | bytes 2359304 | tf_op jit(solution)/shard_map/ppermute | solution.py:414
  1132.4 4.5 copy-start.4
  1132.4 78.0 %collective-permute-start.5 = (bf16[1,512,768]{2,1,0:T(8,128)(2,1)}, bf16[1,512,768]{2,1,0:T(8,128)(2,1)}, u32[]{:S(2)}, u32[]{:S(2)}) collective-permute-start(bf16[1,512,768]{2,1,0:T(8,128)(2,1)} %collective-permute-done.4.refs_2_), channel_id=1, source_target_pairs={{0,1},{1,0},{2,3},{3,2},{4,5},{5,4},{6,7},{7,6}} | collective-permute-start | bytes 2359304 | tf_op jit(solution)/shard_map/ppermute | solution.py:415
  1136.9 2.6 copy-start.5
  1139.6 73.8 %collective-permute-start.2 = (bf16[1,512,768]{2,1,0:T(8,128)(2,1)}, bf16[1,512,768]{2,1,0:T(8,128)(2,1)}, u32[]{:S(2)}, u32[]{:S(2)}) collective-permute-start(bf16[1,512,768]{2,1,0:T(8,128)(2,1)} %get-tuple-element.13.refs_0_), channel_id=1, source_target_pairs={{0,1},{1,0},{2,3},{3,2},{4,5},{5,4},{6,7},{7,6}} | collective-permute-start | bytes 2359304 | tf_op jit(solution)/shard_map/ppermute | solution.py:414
  1204.6 54.6 %collective-permute-start.1 = (bf16[1,512,768]{2,1,0:T(8,128)(2,1)}, bf16[1,512,768]{2,1,0:T(8,128)(2,1)}, u32[]{:S(2)}, u32[]{:S(2)}) collective-permute-start(bf16[1,512,768]{2,1,0:T(8,128)(2,1)} %copy-done.13), channel_id=1, source_target_pairs={{0,1},{1,0},{2,3},{3,2},{4,5},{5,4},{6,7},{7,6}} | collective-permute-start | bytes 2359304 | tf_op jit(solution)/shard_map/ppermute | solution.py:415

commit v3 on v2

--- a/solution.py
+++ b/solution.py
@@ -21,7 +21,7 @@
 GROUP = 4
 CHUNKS = (2, 6, 8, 8, 4, 2, 1, 1)
 FIRSTS = tuple(sum(CHUNKS[:c]) for c in range(len(CHUNKS)))
-PIECES = 4
+PIECES = 8
 ORDER = (2, 3, 1, 0)
 X_PERM = ((0, 2), (1, 3), (2, 0), (3, 1))
 CORE_PERM = ((0, 1), (1, 0), (2, 3), (3, 2))
@@ -61,7 +61,7 @@
         return pltpu.make_async_copy(sbuf.at[slot], dst, st_sem.at[slot])
 
     def send_sum(r, k):
-        return remote(ss_loc.at[r, k - 1], ss_in.at[r, k], s_send.at[r, k - 1], s_recv.at[r, k - 1], k)
+        return remote(ss_loc.at[r, k - 1, pl.ds(0, 1)], ss_in.at[r, k, pl.ds(0, 1)], s_send.at[r, k - 1], s_recv.at[r, k - 1], k)
 
     def send_m(r, k):
         return (remote(mb.at[r, k - 1], xin.at[r, pl.ds(k * rows, rows)], m_send.at[r, k - 1], m_recv.at[r, k - 1], k),
@@ -173,8 +173,8 @@
         fetch = pltpu.make_async_copy(xin.at[r], xa, x_sem)
         fetch.start()
         fetch.wait()
-        total = ss_in[r, 0] + ss_in[r, 1] + ss_in[r, 2] + ss_in[r, 3]
-        denom = (jnp.sqrt(total) + NORM_EPS)[0:1, 0:1]
+        total = sum(ss_in[r, k, 0:1, :] for k in range(1, GROUP)) + ss_in[r, 0, 0:1, :]
+        denom = (jnp.sqrt(total) + NORM_EPS)[:, 0:1]
 
         def scale(i, c):
             sl = pl.ds(pl.multiple_of(i * strip, strip), strip)

time: 1260 us -> 1260 us (level)
  no operation moved by 1% of the time
where the time goes in v3:
time: 1260 us
  Pallas kernels  650 us (52%)
  waiting for transfers between devices  524 us (42%)
  other arithmetic  41.4 us (3%)
  starting transfers between devices  31.7 us (3%)
    pallas_call x1, Pallas kernels, exchange(): pl.pallas_call(functools.partial(exchange_kernel, rounds, rms_scale), out...  571 us
    ppermute x7, waiting for transfers between devices, local_step(): chip.append(lax.ppermute(own[c], 'data', X_PERM))  488 us
    pallas_call x10, Pallas kernels, place(): pl.pallas_call(functools.partial(place_kernel, FIRSTS[chunk], parts), out...  79.7 us
    add x1, other arithmetic, local_step(): mom_new = MOMENTUM * mom_late + grad_late.astype(jnp.float32)  41.4 us
    ppermute x8, waiting for transfers between devices, local_step(): diag.append(lax.ppermute(chip[c], 'data', CORE_PERM))  29.1 us
  transfers between devices with their start and end apart: 23, of which 4 were waited for; matrix products, arithmetic and copies ran while one was open for 3% of the time, Pallas kernels for 6%

profile of v3, /device:TPU:0, one launch (start us, length us, event | category | flops | bytes accessed | tf_op | source)
XLA Modules:
  0.0 1260.0 jit_solution(7254760685756159355)
XLA Ops:
  0.6 570.6 %exchange.1 = (bf16[2,512,768]{2,1,0:T(8,128)(2,1)}, bf16[6,512,768]{2,1,0:T(8,128)(2,1)}, bf16[8,512,768]{2,1,0:T(8,128)(2,1)}, bf16[8,512,768]{2,1,0:T(8,128)(...) custom-call(f32[32,512,768]{2,1,0:T(8,128)} %w_ref.1, ...), custom_call_target="tpu_custom_call" | custom-call | flops 229512314880 | bytes 150994944 | tf_op jit(solution)/shard_map/exchange/pallas_call | solution.py:318
  571.2 0.2 collective-permute-start.4
  571.4 15.9 %collective-permute-start.21 = (bf16[2,512,768]{2,1,0:T(8,128)(2,1)}, bf16[2,512,768]{2,1,0:T(8,128)(2,1)S(1)}, u32[]{:S(2)}, u32[]{:S(2)}) collective-permute-start(bf16[2,512,768]{2,1,0:T(8,128)(2,1)} %get-tuple-element.20.refs_0_), channel_id=1, source_target_pairs={{0,1},{1,0},{2,3},{3,2},{4,5},{5,4},{6,7},{7,6}} | collective-permute-start | bytes 4718600 | tf_op jit(solution)/shard_map/ppermute | solution.py:414
  587.3 0.0 collective-permute-start.22
  587.3 0.8 collective-permute-start.7
  588.1 1.2 collective-permute-start.10
  589.3 0.0 collective-permute-done.4.refs_2_
  589.4 0.8 collective-permute-start
  590.2 118.9 %collective-permute-done.refs_0_ = bf16[1,512,768]{2,1,0:T(8,128)(2,1)S(1)} collective-permute-done((bf16[1,512,768]{2,1,0:T(8,128)(2,1)}, bf16[1,512,768]{2,1,0:T(8,128)(2,1)S(1)}, u32[]{:S(2)}, u32[]{:S(2)}) %collective-permute-start) | collective-permute-done | bytes 786464 | tf_op jit(solution)/shard_map/ppermute | solution.py:412
  709.1 6.3 collective-permute-start.9
  715.4 0.0 collective-permute-done.21.refs_1_
  715.4 1.1 copy-done.11
  716.6 1.2 collective-permute-start.16
  717.8 0.0 collective-permute-done.22.refs_3_
  717.8 1.1 copy-done.12
  718.9 0.8 collective-permute-start.13
  719.7 0.0 collective-permute-done.7.refs_2_
  719.7 1.2 collective-permute-start.19
  721.0 0.0 collective-permute-done.10.refs_2_
  721.0 0.1 collective-permute-start.15
  721.0 0.0 collective-permute-done.9.refs_1_
  721.0 0.4 collective-permute-start.18
  721.5 369.5 %collective-permute-done.19.refs_2_ = bf16[6,512,768]{2,1,0:T(8,128)(2,1)S(1)} collective-permute-done((bf16[6,512,768]{2,1,0:T(8,128)(2,1)}, bf16[6,512,768]{2,1,0:T(8,128)(2,1)S(1)}, u32[]{:S(2)}, u32[]{:S(2)}) %collective-permute-start.19) | collective-permute-done | bytes 4718624 | tf_op jit(solution)/shard_map/ppermute | solution.py:412
  1091.0 0.0 collective-permute-start.12
  1091.1 0.0 collective-permute-done.16.refs_2_
  1091.1 2.7 copy-done
  1093.7 0.7 collective-permute-start.17
  1094.4 0.0 collective-permute-done.13.refs_2_
  1094.4 0.0 collective-permute-start.14
  1094.5 0.0 collective-permute-done.18.refs_1_
  1094.5 0.5 collective-permute-start.20
  1095.0 0.0 collective-permute-done.15.refs_1_
  1095.0 0.0 collective-permute-start.11
  1095.0 6.4 collective-permute-done.12.refs_1_
  1101.4 0.1 collective-permute-start.6
  1101.5 29.1 %collective-permute-done.11.refs_3_ = bf16[4,512,768]{2,1,0:T(8,128)(2,1)S(1)} collective-permute-done((bf16[4,512,768]{2,1,0:T(8,128)(2,1)S(1)}, bf16[4,512,768]{2,1,0:T(8,128)(2,1)S(1)}, u32[]{:S(2)}, u32[]{:S(2)}) %collective-permute-start.11) | collective-permute-done | bytes 3145760 | tf_op jit(solution)/shard_map/ppermute | solution.py:415
  1130.6 0.1 collective-permute-start.8
  1130.8 0.0 collective-permute-done.20.refs_3_
  1130.8 0.4 collective-permute-start.3
  1131.2 0.0 collective-permute-done.17.refs_3_
  1131.2 0.2 collective-permute-start.5
  1131.3 0.0 collective-permute-done.14.refs_3_
  1131.4 1.0 copy-done.10
  1132.3 1.3 copy-done.8
  1133.7 2.0 copy-done.4
  1135.7 2.6 copy-done.5
  1138.3 0.1 collective-permute-start.2
  1138.5 5.5 place.10.refs_4_
  1143.9 13.8 %place.11.refs_4_ = bf16[32,2048,768]{2,1,0:T(8,128)(2,1)} custom-call(bf16[6,512,768]{2,1,0:T(8,128)(2,1)} %get-tuple-element.19.refs_0_, bf16[6,512,768]{2,1,0:T(8,128)(2,1)} %copy-done.7, bf16[6,512,768]{2,1,0:T(8,128)(2,1)} %copy-done.6, bf16[6,512,768]{2,1,0:T(8,128)(2,1)} %copy-done.8, ...), custom_call_target="tpu_custom_call", output_to_operand_aliasing={{}: (4, {})} | custom-call | flops 9437184 | bytes 37748736 | tf_op jit(solution)/shard_map/place/pallas_call | solution.py:389
  1157.7 18.0 %place.12.refs_4_ = bf16[32,2048,768]{2,1,0:T(8,128)(2,1)} custom-call(bf16[8,512,768]{2,1,0:T(8,128)(2,1)} %get-tuple-element.18.refs_0_, bf16[8,512,768]{2,1,0:T(8,128)(2,1)} %copy-done.2, bf16[8,512,768]{2,1,0:T(8,128)(2,1)} %copy-done, bf16[8,512,768]{2,1,0:T(8,128)(2,1)} %copy-done.4, ...), custom_call_target="tpu_custom_call", output_to_operand_aliasing={{}: (4, {})} | custom-call | flops 12582912 | bytes 50331648 | tf_op jit(solution)/shard_map/place/pallas_call | solution.py:389
  1175.7 18.0 %place.13.refs_4_ = bf16[32,2048,768]{2,1,0:T(8,128)(2,1)} custom-call(bf16[8,512,768]{2,1,0:T(8,128)(2,1)} %get-tuple-element.17.refs_0_, bf16[8,512,768]{2,1,0:T(8,128)(2,1)} %copy-done.3, bf16[8,512,768]{2,1,0:T(8,128)(2,1)} %copy-done.1, bf16[8,512,768]{2,1,0:T(8,128)(2,1)} %copy-done.5, ...), custom_call_target="tpu_custom_call", output_to_operand_aliasing={{}: (4, {})} | custom-call | flops 12582912 | bytes 50331648 | tf_op jit(solution)/shard_map/place/pallas_call | solution.py:389
  1193.7 9.6 place.14.refs_4_
  1203.3 0.0 collective-permute-done.6.refs_1_
  1203.3 0.4 collective-permute-start.1
  1203.7 0.0 collective-permute-done.8.refs_3_
  1203.7 5.5 place.15.refs_4_
  1209.2 0.0 collective-permute-done.3.refs_1_
  1209.2 0.0 collective-permute-done.5.refs_3_
  1209.2 2.9 place.16.refs_2_
  1212.2 0.0 collective-permute-done.2.refs_1_
  1212.2 2.3 place.17.refs_1_
  1214.5 41.4 %convert_add_fusion = f32[32,512,768]{2,1,0:T(8,128)} fusion(bf16[32,512,768]{2,1,0:T(8,128)(2,1)} %grad_ref.1, f32[32,512,768]{2,1,0:T(8,128)} %mom_ref.1), kind=kLoop, calls=%fused_computation | loop fusion | flops 37748736 | bytes 125829120 | tf_op jit(solution)/shard_map/add | solution.py:417
  1255.9 2.0 place.18.refs_1_
  1257.9 2.1 place.19
  (22 shorter events, 0.0 us)
Async XLA Ops:
  571.2 18.2 %collective-permute-start.4 = (bf16[1,512,768]{2,1,0:T(8,128)(2,1)}, bf16[1,512,768]{2,1,0:T(8,128)(2,1)}, u32[]{:S(2)}, u32[]{:S(2)}) collective-permute-start(bf16[1,512,768]{2,1,0:T(8,128)(2,1)} %get-tuple-element.14.refs_0_), channel_id=1, source_target_pairs={{0,2},{1,3},{2,0},{3,1},{4,6},{5,7},{6,4},{7,5}} | collective-permute-start | bytes 2359304 | tf_op jit(solution)/shard_map/ppermute | solution.py:412
  571.4 144.0 %collective-permute-start.21 = (bf16[2,512,768]{2,1,0:T(8,128)(2,1)}, bf16[2,512,768]{2,1,0:T(8,128)(2,1)S(1)}, u32[]{:S(2)}, u32[]{:S(2)}) collective-permute-start(bf16[2,512,768]{2,1,0:T(8,128)(2,1)} %get-tuple-element.20.refs_0_), channel_id=1, source_target_pairs={{0,1},{1,0},{2,3},{3,2},{4,5},{5,4},{6,7},{7,6}} | collective-permute-start | bytes 4718600 | tf_op jit(solution)/shard_map/ppermute | solution.py:414
  587.3 130.5 %collective-permute-start.22 = (bf16[2,512,768]{2,1,0:T(8,128)(2,1)}, bf16[2,512,768]{2,1,0:T(8,128)(2,1)S(1)}, u32[]{:S(2)}, u32[]{:S(2)}) collective-permute-start(bf16[2,512,768]{2,1,0:T(8,128)(2,1)} %get-tuple-element.21.refs_2_), channel_id=1, source_target_pairs={{0,1},{1,0},{2,3},{3,2},{4,5},{5,4},{6,7},{7,6}} | collective-permute-start | bytes 4718600 | tf_op jit(solution)/shard_map/ppermute | solution.py:415
  587.3 132.4 %collective-permute-start.7 = (bf16[2,512,768]{2,1,0:T(8,128)(2,1)}, bf16[2,512,768]{2,1,0:T(8,128)(2,1)}, u32[]{:S(2)}, u32[]{:S(2)}) collective-permute-start(bf16[2,512,768]{2,1,0:T(8,128)(2,1)} %get-tuple-element.15.refs_0_), channel_id=1, source_target_pairs={{0,2},{1,3},{2,0},{3,1},{4,6},{5,7},{6,4},{7,5}} | collective-permute-start | bytes 4718600 | tf_op jit(solution)/shard_map/ppermute | solution.py:412
  588.1 132.8 %collective-permute-start.10 = (bf16[4,512,768]{2,1,0:T(8,128)(2,1)}, bf16[4,512,768]{2,1,0:T(8,128)(2,1)S(1)}, u32[]{:S(2)}, u32[]{:S(2)}) collective-permute-start(bf16[4,512,768]{2,1,0:T(8,128)(2,1)} %get-tuple-element.16.refs_0_), channel_id=1, source_target_pairs={{0,2},{1,3},{2,0},{3,1},{4,6},{5,7},{6,4},{7,5}} | collective-permute-start | bytes 9437192 | tf_op jit(solution)/shard_map/ppermute | solution.py:412
  589.4 119.7 %collective-permute-start = (bf16[1,512,768]{2,1,0:T(8,128)(2,1)}, bf16[1,512,768]{2,1,0:T(8,128)(2,1)S(1)}, u32[]{:S(2)}, u32[]{:S(2)}) collective-permute-start(bf16[1,512,768]{2,1,0:T(8,128)(2,1)} %get-tuple-element.13.refs_0_), channel_id=1, source_target_pairs={{0,2},{1,3},{2,0},{3,1},{4,6},{5,7},{6,4},{7,5}} | collective-permute-start | bytes 2359304 | tf_op jit(solution)/shard_map/ppermute | solution.py:412
  709.1 6.4 copy-start.13
  709.1 12.0 collective-permute-start.9
  715.4 1.1 copy-start.11
  716.6 374.5 %collective-permute-start.16 = (bf16[8,512,768]{2,1,0:T(8,128)(2,1)}, bf16[8,512,768]{2,1,0:T(8,128)(2,1)S(1)}, u32[]{:S(2)}, u32[]{:S(2)}) collective-permute-start(bf16[8,512,768]{2,1,0:T(8,128)(2,1)} %get-tuple-element.18.refs_0_), channel_id=1, source_target_pairs={{0,2},{1,3},{2,0},{3,1},{4,6},{5,7},{6,4},{7,5}} | collective-permute-start | bytes 18874376 | tf_op jit(solution)/shard_map/ppermute | solution.py:412
  717.8 1.2 copy-start.12
  718.9 375.5 %collective-permute-start.13 = (bf16[8,512,768]{2,1,0:T(8,128)(2,1)}, bf16[8,512,768]{2,1,0:T(8,128)(2,1)S(1)}, u32[]{:S(2)}, u32[]{:S(2)}) collective-permute-start(bf16[8,512,768]{2,1,0:T(8,128)(2,1)} %get-tuple-element.17.refs_0_), channel_id=1, source_target_pairs={{0,2},{1,3},{2,0},{3,1},{4,6},{5,7},{6,4},{7,5}} | collective-permute-start | bytes 18874376 | tf_op jit(solution)/shard_map/ppermute | solution.py:412
  719.7 371.3 %collective-permute-start.19 = (bf16[6,512,768]{2,1,0:T(8,128)(2,1)}, bf16[6,512,768]{2,1,0:T(8,128)(2,1)S(1)}, u32[]{:S(2)}, u32[]{:S(2)}) collective-permute-start(bf16[6,512,768]{2,1,0:T(8,128)(2,1)} %get-tuple-element.19.refs_0_), channel_id=1, source_target_pairs={{0,2},{1,3},{2,0},{3,1},{4,6},{5,7},{6,4},{7,5}} | collective-permute-start | bytes 14155784 | tf_op jit(solution)/shard_map/ppermute | solution.py:412
  721.0 410.4 %copy-start.9 = (bf16[4,512,768]{2,1,0:T(8,128)(2,1)}, bf16[4,512,768]{2,1,0:T(8,128)(2,1)S(1)}, u32[]{:S(2)}) copy-start(bf16[4,512,768]{2,1,0:T(8,128)(2,1)S(1)} %collective-permute-done.10.refs_2_) | copy-start | bytes 9437188
  721.0 374.0 %collective-permute-start.15 = (bf16[8,512,768]{2,1,0:T(8,128)(2,1)}, bf16[8,512,768]{2,1,0:T(8,128)(2,1)S(1)}, u32[]{:S(2)}, u32[]{:S(2)}) collective-permute-start(bf16[8,512,768]{2,1,0:T(8,128)(2,1)} %get-tuple-element.18.refs_0_), channel_id=1, source_target_pairs={{0,1},{1,0},{2,3},{3,2},{4,5},{5,4},{6,7},{7,6}} | collective-permute-start | bytes 18874376 | tf_op jit(solution)/shard_map/ppermute | solution.py:414
  721.0 373.4 %collective-permute-start.18 = (bf16[6,512,768]{2,1,0:T(8,128)(2,1)}, bf16[6,512,768]{2,1,0:T(8,128)(2,1)S(1)}, u32[]{:S(2)}, u32[]{:S(2)}) collective-permute-start(bf16[6,512,768]{2,1,0:T(8,128)(2,1)} %get-tuple-element.19.refs_0_), channel_id=1, source_target_pairs={{0,1},{1,0},{2,3},{3,2},{4,5},{5,4},{6,7},{7,6}} | collective-permute-start | bytes 14155784 | tf_op jit(solution)/shard_map/ppermute | solution.py:414
  1091.0 40.3 %copy-start.6 = (bf16[6,512,768]{2,1,0:T(8,128)(2,1)}, bf16[6,512,768]{2,1,0:T(8,128)(2,1)S(1)}, u32[]{:S(2)}) copy-start(bf16[6,512,768]{2,1,0:T(8,128)(2,1)S(1)} %collective-permute-done.19.refs_2_) | copy-start | bytes 14155780
  1091.0 10.4 collective-permute-start.12
  1091.1 2.7 copy-start
  1093.7 37.4 %collective-permute-start.17 = (bf16[8,512,768]{2,1,0:T(8,128)(2,1)S(1)}, bf16[8,512,768]{2,1,0:T(8,128)(2,1)S(1)}, u32[]{:S(2)}, u32[]{:S(2)}) collective-permute-start(bf16[8,512,768]{2,1,0:T(8,128)(2,1)S(1)} %collective-permute-done.16.refs_2_), channel_id=1, source_target_pairs={{0,1},{1,0},{2,3},{3,2},{4,5},{5,4},{6,7},{7,6}} | collective-permute-start | bytes 18874376 | tf_op jit(solution)/shard_map/ppermute | solution.py:415
  1094.4 36.7 %copy-start.1 = (bf16[8,512,768]{2,1,0:T(8,128)(2,1)}, bf16[8,512,768]{2,1,0:T(8,128)(2,1)S(1)}, u32[]{:S(2)}) copy-start(bf16[8,512,768]{2,1,0:T(8,128)(2,1)S(1)} %collective-permute-done.13.refs_2_) | copy-start | bytes 18874372
  1094.4 36.9 %collective-permute-start.14 = (bf16[8,512,768]{2,1,0:T(8,128)(2,1)S(1)}, bf16[8,512,768]{2,1,0:T(8,128)(2,1)S(1)}, u32[]{:S(2)}, u32[]{:S(2)}) collective-permute-start(bf16[8,512,768]{2,1,0:T(8,128)(2,1)S(1)} %collective-permute-done.13.refs_2_), channel_id=1, source_target_pairs={{0,1},{1,0},{2,3},{3,2},{4,5},{5,4},{6,7},{7,6}} | collective-permute-start | bytes 18874376 | tf_op jit(solution)/shard_map/ppermute | solution.py:415
  1094.5 36.9 %copy-start.7 = (bf16[6,512,768]{2,1,0:T(8,128)(2,1)}, bf16[6,512,768]{2,1,0:T(8,128)(2,1)S(1)}, u32[]{:S(2)}) copy-start(bf16[6,512,768]{2,1,0:T(8,128)(2,1)S(1)} %collective-permute-done.18.refs_1_) | copy-start | bytes 14155780
  1094.5 36.3 %collective-permute-start.20 = (bf16[6,512,768]{2,1,0:T(8,128)(2,1)S(1)}, bf16[6,512,768]{2,1,0:T(8,128)(2,1)S(1)}, u32[]{:S(2)}, u32[]{:S(2)}) collective-permute-start(bf16[6,512,768]{2,1,0:T(8,128)(2,1)S(1)} %collective-permute-done.19.refs_2_), channel_id=1, source_target_pairs={{0,1},{1,0},{2,3},{3,2},{4,5},{5,4},{6,7},{7,6}} | collective-permute-start | bytes 14155784 | tf_op jit(solution)/shard_map/ppermute | solution.py:415
  1095.0 36.4 %copy-start.2 = (bf16[8,512,768]{2,1,0:T(8,128)(2,1)}, bf16[8,512,768]{2,1,0:T(8,128)(2,1)S(1)}, u32[]{:S(2)}) copy-start(bf16[8,512,768]{2,1,0:T(8,128)(2,1)S(1)} %collective-permute-done.15.refs_1_) | copy-start | bytes 18874372
  1095.0 35.7 %collective-permute-start.11 = (bf16[4,512,768]{2,1,0:T(8,128)(2,1)S(1)}, bf16[4,512,768]{2,1,0:T(8,128)(2,1)S(1)}, u32[]{:S(2)}, u32[]{:S(2)}) collective-permute-start(bf16[4,512,768]{2,1,0:T(8,128)(2,1)S(1)} %collective-permute-done.10.refs_2_), channel_id=1, source_target_pairs={{0,1},{1,0},{2,3},{3,2},{4,5},{5,4},{6,7},{7,6}} | collective-permute-start | bytes 9437192 | tf_op jit(solution)/shard_map/ppermute | solution.py:415
  1101.4 30.0 %copy-start.3 = (bf16[8,512,768]{2,1,0:T(8,128)(2,1)}, bf16[8,512,768]{2,1,0:T(8,128)(2,1)S(1)}, u32[]{:S(2)}) copy-start(bf16[8,512,768]{2,1,0:T(8,128)(2,1)S(1)} %collective-permute-done.12.refs_1_) | copy-start | bytes 18874372
  1101.4 101.9 %collective-permute-start.6 = (bf16[2,512,768]{2,1,0:T(8,128)(2,1)}, bf16[2,512,768]{2,1,0:T(8,128)(2,1)}, u32[]{:S(2)}, u32[]{:S(2)}) collective-permute-start(bf16[2,512,768]{2,1,0:T(8,128)(2,1)} %get-tuple-element.15.refs_0_), channel_id=1, source_target_pairs={{0,1},{1,0},{2,3},{3,2},{4,5},{5,4},{6,7},{7,6}} | collective-permute-start | bytes 4718600 | tf_op jit(solution)/shard_map/ppermute | solution.py:414
  1130.6 1.7 copy-start.10
  1130.6 73.1 %collective-permute-start.8 = (bf16[2,512,768]{2,1,0:T(8,128)(2,1)}, bf16[2,512,768]{2,1,0:T(8,128)(2,1)}, u32[]{:S(2)}, u32[]{:S(2)}) collective-permute-start(bf16[2,512,768]{2,1,0:T(8,128)(2,1)} %collective-permute-done.7.refs_2_), channel_id=1, source_target_pairs={{0,1},{1,0},{2,3},{3,2},{4,5},{5,4},{6,7},{7,6}} | collective-permute-start | bytes 4718600 | tf_op jit(solution)/shard_map/ppermute | solution.py:415
  1130.8 2.9 copy-start.8
  1130.8 78.4 %collective-permute-start.3 = (bf16[1,512,768]{2,1,0:T(8,128)(2,1)}, bf16[1,512,768]{2,1,0:T(8,128)(2,1)}, u32[]{:S(2)}, u32[]{:S(2)}) collective-permute-start(bf16[1,512,768]{2,1,0:T(8,128)(2,1)} %get-tuple-element.14.refs_0_), channel_id=1, source_target_pairs={{0,1},{1,0},{2,3},{3,2},{4,5},{5,4},{6,7},{7,6}} | collective-permute-start | bytes 2359304 | tf_op jit(solution)/shard_map/ppermute | solution.py:414
  1131.2 4.5 copy-start.4
  1131.2 78.0 %collective-permute-start.5 = (bf16[1,512,768]{2,1,0:T(8,128)(2,1)}, bf16[1,512,768]{2,1,0:T(8,128)(2,1)}, u32[]{:S(2)}, u32[]{:S(2)}) collective-permute-start(bf16[1,512,768]{2,1,0:T(8,128)(2,1)} %collective-permute-done.4.refs_2_), channel_id=1, source_target_pairs={{0,1},{1,0},{2,3},{3,2},{4,5},{5,4},{6,7},{7,6}} | collective-permute-start | bytes 2359304 | tf_op jit(solution)/shard_map/ppermute | solution.py:415
  1135.7 2.6 copy-start.5
  1138.3 73.8 %collective-permute-start.2 = (bf16[1,512,768]{2,1,0:T(8,128)(2,1)}, bf16[1,512,768]{2,1,0:T(8,128)(2,1)}, u32[]{:S(2)}, u32[]{:S(2)}) collective-permute-start(bf16[1,512,768]{2,1,0:T(8,128)(2,1)} %get-tuple-element.13.refs_0_), channel_id=1, source_target_pairs={{0,1},{1,0},{2,3},{3,2},{4,5},{5,4},{6,7},{7,6}} | collective-permute-start | bytes 2359304 | tf_op jit(solution)/shard_map/ppermute | solution.py:414
  1203.3 54.6 %collective-permute-start.1 = (bf16[1,512,768]{2,1,0:T(8,128)(2,1)}, bf16[1,512,768]{2,1,0:T(8,128)(2,1)}, u32[]{:S(2)}, u32[]{:S(2)}) collective-permute-start(bf16[1,512,768]{2,1,0:T(8,128)(2,1)} %copy-done.13), channel_id=1, source_target_pairs={{0,1},{1,0},{2,3},{3,2},{4,5},{5,4},{6,7},{7,6}} | collective-permute-start | bytes 2359304 | tf_op jit(solution)/shard_map/ppermute | solution.py:415

commit v4 on v3

--- a/solution.py
+++ b/solution.py
@@ -37,7 +37,7 @@
     w_outs, (w_chip, mb, xin, oo, orv) = refs[:n], refs[n : n + 5]
     (fbuf, hbuf, sbuf, ss_loc, ss_in, xa, xb, amat, bmat, f_sem, h_sem, st_sem, x_sem,
      m_send, m_recv, s_send, s_recv, o_send, o_recv, w_send, w_recv, turn,
-     pf_sem, ph_sem, ps_sem) = refs[n + 5 :]
+     pf_sem, ph_sem, ps_sem, vbuf) = refs[n + 5 :]
     rows, cols = mom_ref.shape[1], mom_ref.shape[2]
     rel = relations(lax.axis_index("data"))
     strip = 64
@@ -114,11 +114,11 @@
                 pltpu.make_async_copy(grad_ref.at[m, pieces[n]], hbuf.at[0, pieces[n]], ph_sem.at[n]))
 
     def stage_piece(n):
-        return pltpu.make_async_copy(sbuf.at[0, pieces[n]], mb.at[0, first - 1, pieces[n]], ps_sem.at[n])
+        return pltpu.make_async_copy(sbuf.at[0, pieces[n]], vbuf.at[pieces[n]], ps_sem.at[n])
 
     def send_piece(n):
         stage_piece(n).wait()
-        remote(mb.at[0, first - 1, pieces[n]], xin.at[0, pl.ds(first * rows + n * height, height)],
+        remote(vbuf.at[pieces[n]], xin.at[0, pl.ds(first * rows + n * height, height)],
                m_send.at[0, first - 1], m_recv.at[0, first - 1], first).start()
 
     for p in range(PIECES):
@@ -333,6 +333,7 @@
             dma((2,)), dma((2,)), dma((2,)), dma,
             *[dma((rounds, 3))] * 6, *[dma((CHUNKS[0],))] * 2, pltpu.SemaphoreType.REGULAR,
             *[dma((PIECES,))] * 3,
+            pltpu.VMEM((rows, cols), half),
         ],
         compiler_params=pltpu.CompilerParams(collective_id=0, has_side_effects=True, vmem_limit_bytes=60 * 1024 * 1024),
         cost_estimate=pl.CostEstimate(flops=flops, bytes_accessed=12 * mats * rows * cols, transcendentals=0),

time: 1260 us -> 1260 us (level)
  transfers between devices with their start and end apart: 23 -> 23, of which waited for: 4 -> 5; matrix products, arithmetic and copies ran while one was open for 3% -> 3% of each run, Pallas kernels for 6% -> 6%
where the time goes in v4:
time: 1260 us
  Pallas kernels  649 us (52%)
  waiting for transfers between devices  524 us (42%)
  other arithmetic  41.4 us (3%)
  starting transfers between devices  32.5 us (3%)
    pallas_call x1, Pallas kernels, exchange(): pl.pallas_call(functools.partial(exchange_kernel, rounds, rms_scale), out...  570 us
    ppermute x7, waiting for transfers between devices, local_step(): chip.append(lax.ppermute(own[c], 'data', X_PERM))  488 us
    pallas_call x10, Pallas kernels, place(): pl.pallas_call(functools.partial(place_kernel, FIRSTS[chunk], parts), out...  79.7 us
    add x1, other arithmetic, local_step(): mom_new = MOMENTUM * mom_late + grad_late.astype(jnp.float32)  41.4 us
    ppermute x8, waiting for transfers between devices, local_step(): diag.append(lax.ppermute(chip[c], 'data', CORE_PERM))  29.1 us
  transfers between devices with their start and end apart: 23, of which 5 were waited for; matrix products, arithmetic and copies ran while one was open for 3% of the time, Pallas kernels for 6%

profile of v4, /device:TPU:0, one launch (start us, length us, event | category | flops | bytes accessed | tf_op | source)
XLA Modules:
  0.0 1259.9 jit_solution(10365120466129347752)
XLA Ops:
  0.6 569.6 %exchange.1 = (bf16[2,512,768]{2,1,0:T(8,128)(2,1)}, bf16[6,512,768]{2,1,0:T(8,128)(2,1)}, bf16[8,512,768]{2,1,0:T(8,128)(2,1)}, bf16[8,512,768]{2,1,0:T(8,128)(...) custom-call(f32[32,512,768]{2,1,0:T(8,128)} %w_ref.1, ...), custom_call_target="tpu_custom_call" | custom-call | flops 229512314880 | bytes 150994944 | tf_op jit(solution)/shard_map/exchange/pallas_call | solution.py:318
  570.2 1.6 collective-permute-start.4
  571.8 15.0 %collective-permute-start.21 = (bf16[2,512,768]{2,1,0:T(8,128)(2,1)}, bf16[2,512,768]{2,1,0:T(8,128)(2,1)S(1)}, u32[]{:S(2)}, u32[]{:S(2)}) collective-permute-start(bf16[2,512,768]{2,1,0:T(8,128)(2,1)} %get-tuple-element.20.refs_0_), channel_id=1, source_target_pairs={{0,1},{1,0},{2,3},{3,2},{4,5},{5,4},{6,7},{7,6}} | collective-permute-start | bytes 4718600 | tf_op jit(solution)/shard_map/ppermute | solution.py:415
  586.8 0.0 collective-permute-start.22
  586.8 1.3 collective-permute-start.7
  588.0 0.8 collective-permute-start.10
  588.8 0.0 collective-permute-done.4.refs_2_
  588.8 1.3 collective-permute-start
  590.1 118.4 %collective-permute-done.refs_0_ = bf16[1,512,768]{2,1,0:T(8,128)(2,1)S(1)} collective-permute-done((bf16[1,512,768]{2,1,0:T(8,128)(2,1)}, bf16[1,512,768]{2,1,0:T(8,128)(2,1)S(1)}, u32[]{:S(2)}, u32[]{:S(2)}) %collective-permute-start) | collective-permute-done | bytes 786464 | tf_op jit(solution)/shard_map/ppermute | solution.py:413
  708.5 6.8 collective-permute-start.9
  715.3 0.0 collective-permute-done.21.refs_1_
  715.3 1.1 copy-done.11
  716.5 0.8 collective-permute-start.16
  717.2 0.0 collective-permute-done.22.refs_3_
  717.2 1.1 copy-done.12
  718.4 1.3 collective-permute-start.13
  719.7 0.0 collective-permute-done.7.refs_2_
  719.7 0.8 collective-permute-start.19
  720.4 0.0 collective-permute-done.10.refs_2_
  720.4 0.1 collective-permute-start.15
  720.5 0.5 collective-permute-done.9.refs_1_
  721.0 0.4 collective-permute-start.18
  721.3 369.6 %collective-permute-done.19.refs_2_ = bf16[6,512,768]{2,1,0:T(8,128)(2,1)S(1)} collective-permute-done((bf16[6,512,768]{2,1,0:T(8,128)(2,1)}, bf16[6,512,768]{2,1,0:T(8,128)(2,1)S(1)}, u32[]{:S(2)}, u32[]{:S(2)}) %collective-permute-start.19) | collective-permute-done | bytes 4718624 | tf_op jit(solution)/shard_map/ppermute | solution.py:413
  1090.9 0.0 collective-permute-start.12
  1091.0 0.0 collective-permute-done.16.refs_2_
  1091.0 2.7 copy-done
  1093.6 0.7 collective-permute-start.17
  1094.4 0.0 collective-permute-done.13.refs_2_
  1094.4 0.0 collective-permute-start.14
  1094.4 0.0 collective-permute-done.18.refs_1_
  1094.4 0.5 collective-permute-start.20
  1094.9 0.0 collective-permute-done.15.refs_1_
  1094.9 0.0 collective-permute-start.11
  1094.9 6.4 collective-permute-done.12.refs_1_
  1101.3 0.1 collective-permute-start.6
  1101.4 29.1 %collective-permute-done.11.refs_3_ = bf16[4,512,768]{2,1,0:T(8,128)(2,1)S(1)} collective-permute-done((bf16[4,512,768]{2,1,0:T(8,128)(2,1)S(1)}, bf16[4,512,768]{2,1,0:T(8,128)(2,1)S(1)}, u32[]{:S(2)}, u32[]{:S(2)}) %collective-permute-start.11) | collective-permute-done | bytes 3145760 | tf_op jit(solution)/shard_map/ppermute | solution.py:416
  1130.6 0.1 collective-permute-start.8
  1130.7 0.0 collective-permute-done.20.refs_3_
  1130.7 0.4 collective-permute-start.3
  1131.1 0.0 collective-permute-done.17.refs_3_
  1131.1 0.2 collective-permute-start.5
  1131.2 0.0 collective-permute-done.14.refs_3_
  1131.3 1.0 copy-done.10
  1132.3 1.3 copy-done.8
  1133.6 2.0 copy-done.4
  1135.6 2.6 copy-done.5
  1138.2 0.1 collective-permute-start.2
  1138.4 5.5 place.10.refs_4_
  1143.8 13.8 %place.11.refs_4_ = bf16[32,2048,768]{2,1,0:T(8,128)(2,1)} custom-call(bf16[6,512,768]{2,1,0:T(8,128)(2,1)} %get-tuple-element.19.refs_0_, bf16[6,512,768]{2,1,0:T(8,128)(2,1)} %copy-done.7, bf16[6,512,768]{2,1,0:T(8,128)(2,1)} %copy-done.6, bf16[6,512,768]{2,1,0:T(8,128)(2,1)} %copy-done.8, ...), custom_call_target="tpu_custom_call", output_to_operand_aliasing={{}: (4, {})} | custom-call | flops 9437184 | bytes 37748736 | tf_op jit(solution)/shard_map/place/pallas_call | solution.py:390
  1157.6 18.0 %place.12.refs_4_ = bf16[32,2048,768]{2,1,0:T(8,128)(2,1)} custom-call(bf16[8,512,768]{2,1,0:T(8,128)(2,1)} %get-tuple-element.18.refs_0_, bf16[8,512,768]{2,1,0:T(8,128)(2,1)} %copy-done.2, bf16[8,512,768]{2,1,0:T(8,128)(2,1)} %copy-done, bf16[8,512,768]{2,1,0:T(8,128)(2,1)} %copy-done.4, ...), custom_call_target="tpu_custom_call", output_to_operand_aliasing={{}: (4, {})} | custom-call | flops 12582912 | bytes 50331648 | tf_op jit(solution)/shard_map/place/pallas_call | solution.py:390
  1175.6 18.0 %place.13.refs_4_ = bf16[32,2048,768]{2,1,0:T(8,128)(2,1)} custom-call(bf16[8,512,768]{2,1,0:T(8,128)(2,1)} %get-tuple-element.17.refs_0_, bf16[8,512,768]{2,1,0:T(8,128)(2,1)} %copy-done.3, bf16[8,512,768]{2,1,0:T(8,128)(2,1)} %copy-done.1, bf16[8,512,768]{2,1,0:T(8,128)(2,1)} %copy-done.5, ...), custom_call_target="tpu_custom_call", output_to_operand_aliasing={{}: (4, {})} | custom-call | flops 12582912 | bytes 50331648 | tf_op jit(solution)/shard_map/place/pallas_call | solution.py:390
  1193.6 9.6 place.14.refs_4_
  1203.2 0.0 collective-permute-done.6.refs_1_
  1203.2 0.4 collective-permute-start.1
  1203.6 0.0 collective-permute-done.8.refs_3_
  1203.6 5.5 place.15.refs_4_
  1209.1 0.0 collective-permute-done.3.refs_1_
  1209.1 0.0 collective-permute-done.5.refs_3_
  1209.1 2.9 place.16.refs_2_
  1212.1 2.3 place.17.refs_1_
  1214.4 41.4 %convert_add_fusion = f32[32,512,768]{2,1,0:T(8,128)} fusion(bf16[32,512,768]{2,1,0:T(8,128)(2,1)} %grad_ref.1, f32[32,512,768]{2,1,0:T(8,128)} %mom_ref.1), kind=kLoop, calls=%fused_computation | loop fusion | flops 37748736 | bytes 125829120 | tf_op jit(solution)/shard_map/add | solution.py:418
  1255.8 2.0 place.18.refs_1_
  1257.8 0.0 collective-permute-done.1.refs_0_
  1257.9 2.1 place.19
  (22 shorter events, 0.0 us)
Async XLA Ops:
  570.2 18.6 %collective-permute-start.4 = (bf16[1,512,768]{2,1,0:T(8,128)(2,1)}, bf16[1,512,768]{2,1,0:T(8,128)(2,1)}, u32[]{:S(2)}, u32[]{:S(2)}) collective-permute-start(bf16[1,512,768]{2,1,0:T(8,128)(2,1)} %get-tuple-element.14.refs_0_), channel_id=1, source_target_pairs={{0,2},{1,3},{2,0},{3,1},{4,6},{5,7},{6,4},{7,5}} | collective-permute-start | bytes 2359304 | tf_op jit(solution)/shard_map/ppermute | solution.py:413
  571.8 143.6 %collective-permute-start.21 = (bf16[2,512,768]{2,1,0:T(8,128)(2,1)}, bf16[2,512,768]{2,1,0:T(8,128)(2,1)S(1)}, u32[]{:S(2)}, u32[]{:S(2)}) collective-permute-start(bf16[2,512,768]{2,1,0:T(8,128)(2,1)} %get-tuple-element.20.refs_0_), channel_id=1, source_target_pairs={{0,1},{1,0},{2,3},{3,2},{4,5},{5,4},{6,7},{7,6}} | collective-permute-start | bytes 4718600 | tf_op jit(solution)/shard_map/ppermute | solution.py:415
  586.8 130.5 %collective-permute-start.22 = (bf16[2,512,768]{2,1,0:T(8,128)(2,1)}, bf16[2,512,768]{2,1,0:T(8,128)(2,1)S(1)}, u32[]{:S(2)}, u32[]{:S(2)}) collective-permute-start(bf16[2,512,768]{2,1,0:T(8,128)(2,1)} %get-tuple-element.21.refs_2_), channel_id=1, source_target_pairs={{0,1},{1,0},{2,3},{3,2},{4,5},{5,4},{6,7},{7,6}} | collective-permute-start | bytes 4718600 | tf_op jit(solution)/shard_map/ppermute | solution.py:416
  586.8 132.9 %collective-permute-start.7 = (bf16[2,512,768]{2,1,0:T(8,128)(2,1)}, bf16[2,512,768]{2,1,0:T(8,128)(2,1)}, u32[]{:S(2)}, u32[]{:S(2)}) collective-permute-start(bf16[2,512,768]{2,1,0:T(8,128)(2,1)} %get-tuple-element.15.refs_0_), channel_id=1, source_target_pairs={{0,2},{1,3},{2,0},{3,1},{4,6},{5,7},{6,4},{7,5}} | collective-permute-start | bytes 4718600 | tf_op jit(solution)/shard_map/ppermute | solution.py:413
  588.0 132.4 %collective-permute-start.10 = (bf16[4,512,768]{2,1,0:T(8,128)(2,1)}, bf16[4,512,768]{2,1,0:T(8,128)(2,1)S(1)}, u32[]{:S(2)}, u32[]{:S(2)}) collective-permute-start(bf16[4,512,768]{2,1,0:T(8,128)(2,1)} %get-tuple-element.16.refs_0_), channel_id=1, source_target_pairs={{0,2},{1,3},{2,0},{3,1},{4,6},{5,7},{6,4},{7,5}} | collective-permute-start | bytes 9437192 | tf_op jit(solution)/shard_map/ppermute | solution.py:413
  588.8 119.7 %collective-permute-start = (bf16[1,512,768]{2,1,0:T(8,128)(2,1)}, bf16[1,512,768]{2,1,0:T(8,128)(2,1)S(1)}, u32[]{:S(2)}, u32[]{:S(2)}) collective-permute-start(bf16[1,512,768]{2,1,0:T(8,128)(2,1)} %get-tuple-element.13.refs_0_), channel_id=1, source_target_pairs={{0,2},{1,3},{2,0},{3,1},{4,6},{5,7},{6,4},{7,5}} | collective-permute-start | bytes 2359304 | tf_op jit(solution)/shard_map/ppermute | solution.py:413
  708.5 6.8 copy-start.13
  708.5 12.4 collective-permute-start.9
  715.3 1.1 copy-start.11
  716.5 374.5 %collective-permute-start.16 = (bf16[8,512,768]{2,1,0:T(8,128)(2,1)}, bf16[8,512,768]{2,1,0:T(8,128)(2,1)S(1)}, u32[]{:S(2)}, u32[]{:S(2)}) collective-permute-start(bf16[8,512,768]{2,1,0:T(8,128)(2,1)} %get-tuple-element.18.refs_0_), channel_id=1, source_target_pairs={{0,2},{1,3},{2,0},{3,1},{4,6},{5,7},{6,4},{7,5}} | collective-permute-start | bytes 18874376 | tf_op jit(solution)/shard_map/ppermute | solution.py:413
  717.2 1.2 copy-start.12
  718.4 376.0 %collective-permute-start.13 = (bf16[8,512,768]{2,1,0:T(8,128)(2,1)}, bf16[8,512,768]{2,1,0:T(8,128)(2,1)S(1)}, u32[]{:S(2)}, u32[]{:S(2)}) collective-permute-start(bf16[8,512,768]{2,1,0:T(8,128)(2,1)} %get-tuple-element.17.refs_0_), channel_id=1, source_target_pairs={{0,2},{1,3},{2,0},{3,1},{4,6},{5,7},{6,4},{7,5}} | collective-permute-start | bytes 18874376 | tf_op jit(solution)/shard_map/ppermute | solution.py:413
  719.7 371.3 %collective-permute-start.19 = (bf16[6,512,768]{2,1,0:T(8,128)(2,1)}, bf16[6,512,768]{2,1,0:T(8,128)(2,1)S(1)}, u32[]{:S(2)}, u32[]{:S(2)}) collective-permute-start(bf16[6,512,768]{2,1,0:T(8,128)(2,1)} %get-tuple-element.19.refs_0_), channel_id=1, source_target_pairs={{0,2},{1,3},{2,0},{3,1},{4,6},{5,7},{6,4},{7,5}} | collective-permute-start | bytes 14155784 | tf_op jit(solution)/shard_map/ppermute | solution.py:413
  720.4 410.8 %copy-start.9 = (bf16[4,512,768]{2,1,0:T(8,128)(2,1)}, bf16[4,512,768]{2,1,0:T(8,128)(2,1)S(1)}, u32[]{:S(2)}) copy-start(bf16[4,512,768]{2,1,0:T(8,128)(2,1)S(1)} %collective-permute-done.10.refs_2_) | copy-start | bytes 9437188
  720.4 374.5 %collective-permute-start.15 = (bf16[8,512,768]{2,1,0:T(8,128)(2,1)}, bf16[8,512,768]{2,1,0:T(8,128)(2,1)S(1)}, u32[]{:S(2)}, u32[]{:S(2)}) collective-permute-start(bf16[8,512,768]{2,1,0:T(8,128)(2,1)} %get-tuple-element.18.refs_0_), channel_id=1, source_target_pairs={{0,1},{1,0},{2,3},{3,2},{4,5},{5,4},{6,7},{7,6}} | collective-permute-start | bytes 18874376 | tf_op jit(solution)/shard_map/ppermute | solution.py:415
  721.0 373.4 %collective-permute-start.18 = (bf16[6,512,768]{2,1,0:T(8,128)(2,1)}, bf16[6,512,768]{2,1,0:T(8,128)(2,1)S(1)}, u32[]{:S(2)}, u32[]{:S(2)}) collective-permute-start(bf16[6,512,768]{2,1,0:T(8,128)(2,1)} %get-tuple-element.19.refs_0_), channel_id=1, source_target_pairs={{0,1},{1,0},{2,3},{3,2},{4,5},{5,4},{6,7},{7,6}} | collective-permute-start | bytes 14155784 | tf_op jit(solution)/shard_map/ppermute | solution.py:415
  1090.9 40.3 %copy-start.6 = (bf16[6,512,768]{2,1,0:T(8,128)(2,1)}, bf16[6,512,768]{2,1,0:T(8,128)(2,1)S(1)}, u32[]{:S(2)}) copy-start(bf16[6,512,768]{2,1,0:T(8,128)(2,1)S(1)} %collective-permute-done.19.refs_2_) | copy-start | bytes 14155780
  1090.9 10.4 collective-permute-start.12
  1091.0 2.7 copy-start
  1093.6 37.4 %collective-permute-start.17 = (bf16[8,512,768]{2,1,0:T(8,128)(2,1)S(1)}, bf16[8,512,768]{2,1,0:T(8,128)(2,1)S(1)}, u32[]{:S(2)}, u32[]{:S(2)}) collective-permute-start(bf16[8,512,768]{2,1,0:T(8,128)(2,1)S(1)} %collective-permute-done.16.refs_2_), channel_id=1, source_target_pairs={{0,1},{1,0},{2,3},{3,2},{4,5},{5,4},{6,7},{7,6}} | collective-permute-start | bytes 18874376 | tf_op jit(solution)/shard_map/ppermute | solution.py:416
  1094.4 36.7 %copy-start.1 = (bf16[8,512,768]{2,1,0:T(8,128)(2,1)}, bf16[8,512,768]{2,1,0:T(8,128)(2,1)S(1)}, u32[]{:S(2)}) copy-start(bf16[8,512,768]{2,1,0:T(8,128)(2,1)S(1)} %collective-permute-done.13.refs_2_) | copy-start | bytes 18874372
  1094.4 36.9 %collective-permute-start.14 = (bf16[8,512,768]{2,1,0:T(8,128)(2,1)S(1)}, bf16[8,512,768]{2,1,0:T(8,128)(2,1)S(1)}, u32[]{:S(2)}, u32[]{:S(2)}) collective-permute-start(bf16[8,512,768]{2,1,0:T(8,128)(2,1)S(1)} %collective-permute-done.13.refs_2_), channel_id=1, source_target_pairs={{0,1},{1,0},{2,3},{3,2},{4,5},{5,4},{6,7},{7,6}} | collective-permute-start | bytes 18874376 | tf_op jit(solution)/shard_map/ppermute | solution.py:416
  1094.4 36.9 %copy-start.7 = (bf16[6,512,768]{2,1,0:T(8,128)(2,1)}, bf16[6,512,768]{2,1,0:T(8,128)(2,1)S(1)}, u32[]{:S(2)}) copy-start(bf16[6,512,768]{2,1,0:T(8,128)(2,1)S(1)} %collective-permute-done.18.refs_1_) | copy-start | bytes 14155780
  1094.4 36.3 %collective-permute-start.20 = (bf16[6,512,768]{2,1,0:T(8,128)(2,1)S(1)}, bf16[6,512,768]{2,1,0:T(8,128)(2,1)S(1)}, u32[]{:S(2)}, u32[]{:S(2)}) collective-permute-start(bf16[6,512,768]{2,1,0:T(8,128)(2,1)S(1)} %collective-permute-done.19.refs_2_), channel_id=1, source_target_pairs={{0,1},{1,0},{2,3},{3,2},{4,5},{5,4},{6,7},{7,6}} | collective-permute-start | bytes 14155784 | tf_op jit(solution)/shard_map/ppermute | solution.py:416
  1094.9 36.4 %copy-start.2 = (bf16[8,512,768]{2,1,0:T(8,128)(2,1)}, bf16[8,512,768]{2,1,0:T(8,128)(2,1)S(1)}, u32[]{:S(2)}) copy-start(bf16[8,512,768]{2,1,0:T(8,128)(2,1)S(1)} %collective-permute-done.15.refs_1_) | copy-start | bytes 18874372
  1094.9 35.7 %collective-permute-start.11 = (bf16[4,512,768]{2,1,0:T(8,128)(2,1)S(1)}, bf16[4,512,768]{2,1,0:T(8,128)(2,1)S(1)}, u32[]{:S(2)}, u32[]{:S(2)}) collective-permute-start(bf16[4,512,768]{2,1,0:T(8,128)(2,1)S(1)} %collective-permute-done.10.refs_2_), channel_id=1, source_target_pairs={{0,1},{1,0},{2,3},{3,2},{4,5},{5,4},{6,7},{7,6}} | collective-permute-start | bytes 9437192 | tf_op jit(solution)/shard_map/ppermute | solution.py:416
  1101.3 30.0 %copy-start.3 = (bf16[8,512,768]{2,1,0:T(8,128)(2,1)}, bf16[8,512,768]{2,1,0:T(8,128)(2,1)S(1)}, u32[]{:S(2)}) copy-start(bf16[8,512,768]{2,1,0:T(8,128)(2,1)S(1)} %collective-permute-done.12.refs_1_) | copy-start | bytes 18874372
  1101.3 101.9 %collective-permute-start.6 = (bf16[2,512,768]{2,1,0:T(8,128)(2,1)}, bf16[2,512,768]{2,1,0:T(8,128)(2,1)}, u32[]{:S(2)}, u32[]{:S(2)}) collective-permute-start(bf16[2,512,768]{2,1,0:T(8,128)(2,1)} %get-tuple-element.15.refs_0_), channel_id=1, source_target_pairs={{0,1},{1,0},{2,3},{3,2},{4,5},{5,4},{6,7},{7,6}} | collective-permute-start | bytes 4718600 | tf_op jit(solution)/shard_map/ppermute | solution.py:415
  1130.6 1.7 copy-start.10
  1130.6 73.1 %collective-permute-start.8 = (bf16[2,512,768]{2,1,0:T(8,128)(2,1)}, bf16[2,512,768]{2,1,0:T(8,128)(2,1)}, u32[]{:S(2)}, u32[]{:S(2)}) collective-permute-start(bf16[2,512,768]{2,1,0:T(8,128)(2,1)} %collective-permute-done.7.refs_2_), channel_id=1, source_target_pairs={{0,1},{1,0},{2,3},{3,2},{4,5},{5,4},{6,7},{7,6}} | collective-permute-start | bytes 4718600 | tf_op jit(solution)/shard_map/ppermute | solution.py:416
  1130.7 2.9 copy-start.8
  1130.7 78.4 %collective-permute-start.3 = (bf16[1,512,768]{2,1,0:T(8,128)(2,1)}, bf16[1,512,768]{2,1,0:T(8,128)(2,1)}, u32[]{:S(2)}, u32[]{:S(2)}) collective-permute-start(bf16[1,512,768]{2,1,0:T(8,128)(2,1)} %get-tuple-element.14.refs_0_), channel_id=1, source_target_pairs={{0,1},{1,0},{2,3},{3,2},{4,5},{5,4},{6,7},{7,6}} | collective-permute-start | bytes 2359304 | tf_op jit(solution)/shard_map/ppermute | solution.py:415
  1131.1 4.5 copy-start.4
  1131.1 78.0 %collective-permute-start.5 = (bf16[1,512,768]{2,1,0:T(8,128)(2,1)}, bf16[1,512,768]{2,1,0:T(8,128)(2,1)}, u32[]{:S(2)}, u32[]{:S(2)}) collective-permute-start(bf16[1,512,768]{2,1,0:T(8,128)(2,1)} %collective-permute-done.4.refs_2_), channel_id=1, source_target_pairs={{0,1},{1,0},{2,3},{3,2},{4,5},{5,4},{6,7},{7,6}} | collective-permute-start | bytes 2359304 | tf_op jit(solution)/shard_map/ppermute | solution.py:416
  1135.6 2.6 copy-start.5
  1138.2 73.8 %collective-permute-start.2 = (bf16[1,512,768]{2,1,0:T(8,128)(2,1)}, bf16[1,512,768]{2,1,0:T(8,128)(2,1)}, u32[]{:S(2)}, u32[]{:S(2)}) collective-permute-start(bf16[1,512,768]{2,1,0:T(8,128)(2,1)} %get-tuple-element.13.refs_0_), channel_id=1, source_target_pairs={{0,1},{1,0},{2,3},{3,2},{4,5},{5,4},{6,7},{7,6}} | collective-permute-start | bytes 2359304 | tf_op jit(solution)/shard_map/ppermute | solution.py:415
  1203.2 54.6 %collective-permute-start.1 = (bf16[1,512,768]{2,1,0:T(8,128)(2,1)}, bf16[1,512,768]{2,1,0:T(8,128)(2,1)}, u32[]{:S(2)}, u32[]{:S(2)}) collective-permute-start(bf16[1,512,768]{2,1,0:T(8,128)(2,1)} %copy-done.13), channel_id=1, source_target_pairs={{0,1},{1,0},{2,3},{3,2},{4,5},{5,4},{6,7},{7,6}} | collective-permute-start | bytes 2359304 | tf_op jit(solution)/shard_map/ppermute | solution.py:416

commit v5 on v4

--- a/solution.py
+++ b/solution.py
@@ -33,7 +33,7 @@
 
 
 def exchange_kernel(rounds, rms_scale, w_ref, mom_ref, grad_ref, *refs):
-    n = len(CHUNKS)
+    n = len(CHUNKS) + 1
     w_outs, (w_chip, mb, xin, oo, orv) = refs[:n], refs[n : n + 5]
     (fbuf, hbuf, sbuf, ss_loc, ss_in, xa, xb, amat, bmat, f_sem, h_sem, st_sem, x_sem,
      m_send, m_recv, s_send, s_recv, o_send, o_recv, w_send, w_recv, turn,
@@ -262,7 +262,12 @@
         for c in range(len(CHUNKS)):
             @pl.when((m >= FIRSTS[c]) & (m < FIRSTS[c] + CHUNKS[c]))
             def _():
-                stage_w(c, m - FIRSTS[c], slot).start()
+                if c + 1 < len(CHUNKS):
+                    stage_w(c, m - FIRSTS[c], slot).start()
+                else:
+                    for h in range(2):
+                        part_rows = sbuf.at[slot, pl.ds(h * rows // 2, rows // 2)]
+                        pltpu.make_async_copy(part_rows, w_outs[c + h].at[0], st_sem.at[slot]).start()
 
         @pl.when((lax.rem(later, GROUP) == 0) & (later < mats))
         def _():
@@ -307,7 +312,8 @@
     rounds = mats // GROUP
     half, full = jnp.bfloat16, jnp.float32
     rms_scale = 0.2 * math.sqrt(max(rows * GROUP, cols))
-    shapes = [jax.ShapeDtypeStruct((count, rows, cols), half) for count in CHUNKS + CHUNKS[:1]] + [
+    shapes = [jax.ShapeDtypeStruct((count, rows, cols), half) for count in CHUNKS[:-1]] + [
+        jax.ShapeDtypeStruct((1, rows // 2, cols), half)] * 2 + [jax.ShapeDtypeStruct((CHUNKS[0], rows, cols), half)] + [
         jax.ShapeDtypeStruct((rounds, 3, rows, cols), half),
         jax.ShapeDtypeStruct((rounds, GROUP * rows, cols), half),
         jax.ShapeDtypeStruct((rounds, GROUP * rows, cols), half),
@@ -339,10 +345,10 @@
         cost_estimate=pl.CostEstimate(flops=flops, bytes_accessed=12 * mats * rows * cols, transcendentals=0),
         name="exchange",
     )(w_rows, mom_rows, grad_rows)
-    return outs[: len(CHUNKS)], outs[len(CHUNKS)]
-
-
-def place_kernel(first, parts, *refs):
+    return outs[: len(CHUNKS) + 1], outs[len(CHUNKS) + 1]
+
+
+def place_kernel(first, parts, height, offset, *refs):
     blocks, (out_ref, buf, in_sem, out_sem) = refs[: len(parts)], refs[-4:]
     count, rows, _ = blocks[0].shape
     rel = relations(lax.axis_index("data"))
@@ -351,7 +357,7 @@
         return pltpu.make_async_copy(blocks[n].at[i], buf.at[slot, n], in_sem.at[slot, n])
 
     def put(i, n, slot):
-        dst = out_ref.at[first + i, pl.ds(pl.multiple_of(rel[parts[n]] * rows, rows), rows)]
+        dst = out_ref.at[first + i, pl.ds(pl.multiple_of(rel[parts[n]] * height + offset, rows), rows)]
         return pltpu.make_async_copy(buf.at[slot, n], dst, out_sem.at[slot, n])
 
     for n in range(len(parts)):
@@ -378,7 +384,7 @@
         put(count - 1, n, (count - 1) % 2).wait()
 
 
-def place(chunk, blocks, dst, mats):
+def place(first, blocks, dst, mats, height, offset=0):
     parts = tuple(blocks)
     count, rows, cols = blocks[parts[0]].shape
     args, aliases = [blocks[k] for k in parts], {}
@@ -388,8 +394,8 @@
     size = len(parts) * count * rows * cols
     dma = pltpu.SemaphoreType.DMA
     return pl.pallas_call(
-        functools.partial(place_kernel, FIRSTS[chunk], parts),
-        out_shape=jax.ShapeDtypeStruct((mats, rows * GROUP, cols), jnp.bfloat16),
+        functools.partial(place_kernel, first, parts, height, offset),
+        out_shape=jax.ShapeDtypeStruct((mats, height * GROUP, cols), jnp.bfloat16),
         in_specs=[pl.BlockSpec(memory_space=pltpu.HBM)] * len(args),
         out_specs=pl.BlockSpec(memory_space=pltpu.HBM),
         scratch_shapes=[pltpu.VMEM((2, len(parts), rows, cols), jnp.bfloat16), dma((2, len(parts))), dma((2, len(parts)))],
@@ -403,10 +409,10 @@
 def solution(mesh):
     row_spec = P("stage", "data", None)
     full_spec = P("stage", None, None)
-    last = len(CHUNKS) - 1
+    last = len(CHUNKS)
 
     def local_step(w_rows, mom_rows, grad_rows):
-        mats = mom_rows.shape[0]
+        mats, height, _ = mom_rows.shape
         own, w_chip = exchange(w_rows, mom_rows, grad_rows)
         chip, core, diag = [w_chip], [], []
         for c in range(1, last + 1):
@@ -417,11 +423,16 @@
         mom_late, grad_late, _ = lax.optimization_barrier((mom_rows, grad_rows, own[0]))
         mom_new = MOMENTUM * mom_late + grad_late.astype(jnp.float32)
         params = None
-        for c in range(last):
-            params = place(c, {0: own[c], 1: core[c], 2: chip[c], 3: diag[c]}, params, mats)
-        params = place(last, {0: own[last], 1: core[last]}, params, mats)
-        params = place(last, {2: chip[last]}, params, mats)
-        params = place(last, {3: diag[last]}, params, mats)
+
+        def whole(c):
+            return {0: own[c], 1: core[c], 2: chip[c], 3: diag[c]}
+
+        for c in range(last - 1):
+            params = place(FIRSTS[c], whole(c), params, mats, height)
+        params = place(mats - 1, {0: own[last], 1: core[last]}, params, mats, height, height // 2)
+        params = place(mats - 1, whole(last - 1), params, mats, height)
+        params = place(mats - 1, {2: chip[last]}, params, mats, height, height // 2)
+        params = place(mats - 1, {3: diag[last]}, params, mats, height, height // 2)
         return params, mom_new
 
     return jax.shard_map(local_step, mesh=mesh, in_specs=(row_spec, row_spec, row_spec), out_specs=(full_spec, row_spec), check_vma=False)

time: 1260 us -> 1270 us (level)
  waiting for transfers between devices: 524 us -> 537 us
    ppermute x7 -> x8, waiting for transfers between devices: 488 us -> 496 us  [local_step(): chip.append(lax.ppermute(own[c], 'data', X_PERM))]
    pallas_call x10 -> x11, Pallas kernels: 79.7 us -> 81 us  [place(): pl.pallas_call(functools.partial(place_kernel, first, parts, height, offs...]
    ppermute x8 -> x9, waiting for transfers between devices: 29.1 us -> 29.7 us  [local_step(): diag.append(lax.ppermute(chip[c], 'data', CORE_PERM))]
  transfers between devices with their start and end apart: 23 -> 26, of which waited for: 5 -> 9; matrix products, arithmetic and copies ran while one was open for 3% -> 3% of each run, Pallas kernels for 6% -> 6%
where the time goes in v5:
time: 1270 us; the launch traced here: 1260 us
  Pallas kernels  651 us (51%)
  waiting for transfers between devices  537 us (42%)
  other arithmetic  41.4 us (3%)
  starting transfers between devices  22.6 us (2%)
    pallas_call x1, Pallas kernels, exchange(): pl.pallas_call(functools.partial(exchange_kernel, rounds, rms_scale), out...  570 us
    ppermute x8, waiting for transfers between devices, local_step(): chip.append(lax.ppermute(own[c], 'data', X_PERM))  496 us
    pallas_call x11, Pallas kernels, place(): pl.pallas_call(functools.partial(place_kernel, first, parts, height, offs...  81 us
    add x1, other arithmetic, local_step(): mom_new = MOMENTUM * mom_late + grad_late.astype(jnp.float32)  41.4 us
    ppermute x9, waiting for transfers between devices, local_step(): diag.append(lax.ppermute(chip[c], 'data', CORE_PERM))  29.7 us
  transfers between devices with their start and end apart: 26, of which 9 were waited for; matrix products, arithmetic and copies ran while one was open for 3% of the time, Pallas kernels for 6%

profile of v5, /device:TPU:0, one launch (start us, length us, event | category | flops | bytes accessed | tf_op | source)
XLA Modules:
  0.0 1263.1 jit_solution(18292078069289373644)
XLA Ops:
  0.6 569.6 %exchange.1 = (bf16[2,512,768]{2,1,0:T(8,128)(2,1)}, bf16[6,512,768]{2,1,0:T(8,128)(2,1)}, bf16[8,512,768]{2,1,0:T(8,128)(2,1)}, bf16[8,512,768]{2,1,0:T(8,128)(...) custom-call(f32[32,512,768]{2,1,0:T(8,128)} %w_ref.1, ...), custom_call_target="tpu_custom_call" | custom-call | flops 229512314880 | bytes 150994944 | tf_op jit(solution)/shard_map/exchange/pallas_call | solution.py:324
  570.2 10.6 collective-permute-start.24
  580.8 1.2 collective-permute-start.3
  582.0 0.9 collective-permute-start
  582.9 1.2 collective-permute-start.13
  584.0 0.0 collective-permute-start.25
  584.0 9.1 collective-permute-done.3.refs_2_
  593.1 1.2 collective-permute-start.10
  594.3 7.2 collective-permute-done.refs_0_
  601.5 1.2 collective-permute-start.7
  602.6 116.0 %collective-permute-done.7.refs_2_ = bf16[1,512,768]{2,1,0:T(8,128)(2,1)} collective-permute-done((bf16[1,512,768]{2,1,0:T(8,128)(2,1)}, bf16[1,512,768]{2,1,0:T(8,128)(2,1)}, u32[]{:S(2)}, u32[]{:S(2)}) %collective-permute-start.7) | collective-permute-done | bytes 786464 | tf_op jit(solution)/shard_map/ppermute | solution.py:419
  718.6 0.0 collective-permute-start.9
  718.6 0.0 collective-permute-done.24.refs_1_
  718.6 0.5 collective-permute-start.12
  719.1 0.0 collective-permute-done.25.refs_3_
  719.1 1.2 collective-permute-start.19
  720.3 0.0 collective-permute-done.10.refs_2_
  720.3 0.9 collective-permute-start.16
  721.2 1.1 collective-permute-done.9.refs_1_
  722.2 1.2 collective-permute-start.22
  723.4 0.0 collective-permute-done.13.refs_2_
  723.4 0.0 collective-permute-start.11
  723.4 3.3 collective-permute-done.12.refs_1_
  726.7 0.1 collective-permute-start.18
  726.9 1.5 copy-done.10
  728.4 0.6 collective-permute-done.11.refs_3_
  729.0 0.1 collective-permute-start.21
  729.1 363.6 %collective-permute-done.22.refs_2_ = bf16[6,512,768]{2,1,0:T(8,128)(2,1)S(1)} collective-permute-done((bf16[6,512,768]{2,1,0:T(8,128)(2,1)}, bf16[6,512,768]{2,1,0:T(8,128)(2,1)S(1)}, u32[]{:S(2)}, u32[]{:S(2)}) %collective-permute-start.22) | collective-permute-done | bytes 4718624 | tf_op jit(solution)/shard_map/ppermute | solution.py:419
  1092.7 0.0 collective-permute-start.15
  1092.8 0.0 collective-permute-done.19.refs_2_
  1092.8 2.7 copy-done
  1095.4 0.6 collective-permute-start.20
  1096.0 0.0 collective-permute-done.16.refs_2_
  1096.0 0.0 collective-permute-start.17
  1096.0 0.5 collective-permute-start.23
  1096.5 0.0 collective-permute-done.18.refs_1_
  1096.5 0.0 collective-permute-start.14
  1096.6 6.5 collective-permute-done.15.refs_1_
  1103.1 0.1 collective-permute-start.6
  1103.3 29.1 %collective-permute-done.14.refs_3_ = bf16[4,512,768]{2,1,0:T(8,128)(2,1)S(1)} collective-permute-done((bf16[4,512,768]{2,1,0:T(8,128)(2,1)S(1)}, bf16[4,512,768]{2,1,0:T(8,128)(2,1)S(1)}, u32[]{:S(2)}, u32[]{:S(2)}) %collective-permute-start.14) | collective-permute-done | bytes 3145760 | tf_op jit(solution)/shard_map/ppermute | solution.py:422
  1132.4 0.1 collective-permute-start.8
  1132.5 0.0 collective-permute-done.23.refs_3_
  1132.5 0.4 collective-permute-start.5
  1132.9 0.2 collective-permute-start.2
  1133.1 1.0 copy-done.11
  1134.1 1.3 copy-done.8
  1135.4 2.0 copy-done.4
  1137.4 2.6 copy-done.5
  1140.1 0.1 collective-permute-start.4
  1140.2 5.5 place.11.refs_4_
  1145.7 13.8 %place.12.refs_4_ = bf16[32,2048,768]{2,1,0:T(8,128)(2,1)} custom-call(bf16[6,512,768]{2,1,0:T(8,128)(2,1)} %get-tuple-element.21.refs_0_, bf16[6,512,768]{2,1,0:T(8,128)(2,1)} %copy-done.7, bf16[6,512,768]{2,1,0:T(8,128)(2,1)} %copy-done.6, bf16[6,512,768]{2,1,0:T(8,128)(2,1)} %copy-done.8, ...), custom_call_target="tpu_custom_call", output_to_operand_aliasing={{}: (4, {})} | custom-call | flops 9437184 | bytes 37748736 | tf_op jit(solution)/shard_map/place/pallas_call | solution.py:396
  1159.4 18.0 %place.13.refs_4_ = bf16[32,2048,768]{2,1,0:T(8,128)(2,1)} custom-call(bf16[8,512,768]{2,1,0:T(8,128)(2,1)} %get-tuple-element.20.refs_0_, bf16[8,512,768]{2,1,0:T(8,128)(2,1)} %copy-done.2, bf16[8,512,768]{2,1,0:T(8,128)(2,1)} %copy-done, bf16[8,512,768]{2,1,0:T(8,128)(2,1)} %copy-done.4, ...), custom_call_target="tpu_custom_call", output_to_operand_aliasing={{}: (4, {})} | custom-call | flops 12582912 | bytes 50331648 | tf_op jit(solution)/shard_map/place/pallas_call | solution.py:396
  1177.4 18.0 %place.14.refs_4_ = bf16[32,2048,768]{2,1,0:T(8,128)(2,1)} custom-call(bf16[8,512,768]{2,1,0:T(8,128)(2,1)} %get-tuple-element.19.refs_0_, bf16[8,512,768]{2,1,0:T(8,128)(2,1)} %copy-done.3, bf16[8,512,768]{2,1,0:T(8,128)(2,1)} %copy-done.1, bf16[8,512,768]{2,1,0:T(8,128)(2,1)} %copy-done.5, ...), custom_call_target="tpu_custom_call", output_to_operand_aliasing={{}: (4, {})} | custom-call | flops 12582912 | bytes 50331648 | tf_op jit(solution)/shard_map/place/pallas_call | solution.py:396
  1195.4 9.6 place.15.refs_4_
  1205.0 5.5 place.16.refs_4_
  1210.5 0.4 collective-permute-start.1
  1210.9 0.0 collective-permute-done.8.refs_3_
  1210.9 2.9 place.17.refs_2_
  1213.9 1.9 place.18.refs_4_
  1215.8 0.0 collective-permute-done.4.refs_3_
  1215.9 2.3 place.19.refs_1_
  1218.1 41.4 %convert_add_fusion = f32[32,512,768]{2,1,0:T(8,128)} fusion(bf16[32,512,768]{2,1,0:T(8,128)(2,1)} %grad_ref.1, f32[32,512,768]{2,1,0:T(8,128)} %mom_ref.1), kind=kLoop, calls=%fused_computation | loop fusion | flops 37748736 | bytes 125829120 | tf_op jit(solution)/shard_map/add | solution.py:424
  1259.5 1.8 place.20.refs_1_
  1261.3 1.8 place.21
  (37 shorter events, 0.1 us)
Async XLA Ops:
  570.2 148.4 %collective-permute-start.24 = (bf16[2,512,768]{2,1,0:T(8,128)(2,1)}, bf16[2,512,768]{2,1,0:T(8,128)(2,1)S(1)}, u32[]{:S(2)}, u32[]{:S(2)}) collective-permute-start(bf16[2,512,768]{2,1,0:T(8,128)(2,1)} %get-tuple-element.22.refs_0_), channel_id=1, source_target_pairs={{0,1},{1,0},{2,3},{3,2},{4,5},{5,4},{6,7},{7,6}} | collective-permute-start | bytes 4718600 | tf_op jit(solution)/shard_map/ppermute | solution.py:421
  580.8 12.3 collective-permute-start.3
  582.0 19.5 %collective-permute-start = (bf16[1,256,768]{2,1,0:T(8,128)(2,1)}, bf16[1,256,768]{2,1,0:T(8,128)(2,1)S(1)}, u32[]{:S(2)}, u32[]{:S(2)}) collective-permute-start(bf16[1,256,768]{2,1,0:T(8,128)(2,1)} %get-tuple-element.14.refs_0_), channel_id=1, source_target_pairs={{0,2},{1,3},{2,0},{3,1},{4,6},{5,7},{6,4},{7,5}} | collective-permute-start | bytes 1179656 | tf_op jit(solution)/shard_map/ppermute | solution.py:419
  582.9 140.5 %collective-permute-start.13 = (bf16[4,512,768]{2,1,0:T(8,128)(2,1)}, bf16[4,512,768]{2,1,0:T(8,128)(2,1)S(1)}, u32[]{:S(2)}, u32[]{:S(2)}) collective-permute-start(bf16[4,512,768]{2,1,0:T(8,128)(2,1)} %get-tuple-element.18.refs_0_), channel_id=1, source_target_pairs={{0,2},{1,3},{2,0},{3,1},{4,6},{5,7},{6,4},{7,5}} | collective-permute-start | bytes 9437192 | tf_op jit(solution)/shard_map/ppermute | solution.py:419
  584.0 135.1 %collective-permute-start.25 = (bf16[2,512,768]{2,1,0:T(8,128)(2,1)}, bf16[2,512,768]{2,1,0:T(8,128)(2,1)S(1)}, u32[]{:S(2)}, u32[]{:S(2)}) collective-permute-start(bf16[2,512,768]{2,1,0:T(8,128)(2,1)} %get-tuple-element.23.refs_2_), channel_id=1, source_target_pairs={{0,1},{1,0},{2,3},{3,2},{4,5},{5,4},{6,7},{7,6}} | collective-permute-start | bytes 4718600 | tf_op jit(solution)/shard_map/ppermute | solution.py:422
  593.1 127.1 %collective-permute-start.10 = (bf16[2,512,768]{2,1,0:T(8,128)(2,1)}, bf16[2,512,768]{2,1,0:T(8,128)(2,1)S(1)}, u32[]{:S(2)}, u32[]{:S(2)}) collective-permute-start(bf16[2,512,768]{2,1,0:T(8,128)(2,1)} %get-tuple-element.17.refs_0_), channel_id=1, source_target_pairs={{0,2},{1,3},{2,0},{3,1},{4,6},{5,7},{6,4},{7,5}} | collective-permute-start | bytes 4718600 | tf_op jit(solution)/shard_map/ppermute | solution.py:419
  601.5 1.2 copy-start.17
  601.5 117.1 %collective-permute-start.7 = (bf16[1,512,768]{2,1,0:T(8,128)(2,1)}, bf16[1,512,768]{2,1,0:T(8,128)(2,1)}, u32[]{:S(2)}, u32[]{:S(2)}) collective-permute-start(bf16[1,512,768]{2,1,0:T(8,128)(2,1)} %get-tuple-element.16.refs_0_), channel_id=1, source_target_pairs={{0,2},{1,3},{2,0},{3,1},{4,6},{5,7},{6,4},{7,5}} | collective-permute-start | bytes 2359304 | tf_op jit(solution)/shard_map/ppermute | solution.py:419
  718.6 3.6 collective-permute-start.9
  718.6 4.8 copy-start.15
  718.6 8.1 collective-permute-start.12
  719.1 376.9 %copy-start.16 = (bf16[2,512,768]{2,1,0:T(8,128)(2,1)}, bf16[2,512,768]{2,1,0:T(8,128)(2,1)S(1)}, u32[]{:S(2)}) copy-start(bf16[2,512,768]{2,1,0:T(8,128)(2,1)S(1)} %collective-permute-done.25.refs_3_) | copy-start | bytes 4718596
  719.1 373.6 %collective-permute-start.19 = (bf16[8,512,768]{2,1,0:T(8,128)(2,1)}, bf16[8,512,768]{2,1,0:T(8,128)(2,1)S(1)}, u32[]{:S(2)}, u32[]{:S(2)}) collective-permute-start(bf16[8,512,768]{2,1,0:T(8,128)(2,1)} %get-tuple-element.20.refs_0_), channel_id=1, source_target_pairs={{0,2},{1,3},{2,0},{3,1},{4,6},{5,7},{6,4},{7,5}} | collective-permute-start | bytes 18874376 | tf_op jit(solution)/shard_map/ppermute | solution.py:419
  720.3 6.6 copy-start.12
  720.3 375.7 %collective-permute-start.16 = (bf16[8,512,768]{2,1,0:T(8,128)(2,1)}, bf16[8,512,768]{2,1,0:T(8,128)(2,1)S(1)}, u32[]{:S(2)}, u32[]{:S(2)}) collective-permute-start(bf16[8,512,768]{2,1,0:T(8,128)(2,1)} %get-tuple-element.19.refs_0_), channel_id=1, source_target_pairs={{0,2},{1,3},{2,0},{3,1},{4,6},{5,7},{6,4},{7,5}} | collective-permute-start | bytes 18874376 | tf_op jit(solution)/shard_map/ppermute | solution.py:419
  722.2 373.8 %copy-start.13 = (bf16[2,512,768]{2,1,0:T(8,128)(2,1)}, bf16[2,512,768]{2,1,0:T(8,128)(2,1)S(1)}, u32[]{:S(2)}) copy-start(bf16[2,512,768]{2,1,0:T(8,128)(2,1)S(1)} %collective-permute-done.9.refs_1_) | copy-start | bytes 4718596
  722.2 370.5 %collective-permute-start.22 = (bf16[6,512,768]{2,1,0:T(8,128)(2,1)}, bf16[6,512,768]{2,1,0:T(8,128)(2,1)S(1)}, u32[]{:S(2)}, u32[]{:S(2)}) collective-permute-start(bf16[6,512,768]{2,1,0:T(8,128)(2,1)} %get-tuple-element.21.refs_0_), channel_id=1, source_target_pairs={{0,2},{1,3},{2,0},{3,1},{4,6},{5,7},{6,4},{7,5}} | collective-permute-start | bytes 14155784 | tf_op jit(solution)/shard_map/ppermute | solution.py:419
  723.4 409.7 %copy-start.9 = (bf16[4,512,768]{2,1,0:T(8,128)(2,1)}, bf16[4,512,768]{2,1,0:T(8,128)(2,1)S(1)}, u32[]{:S(2)}) copy-start(bf16[4,512,768]{2,1,0:T(8,128)(2,1)S(1)} %collective-permute-done.13.refs_2_) | copy-start | bytes 9437188
  723.4 5.6 collective-permute-start.11
  726.7 1.6 copy-start.10
  726.7 369.8 %collective-permute-start.18 = (bf16[8,512,768]{2,1,0:T(8,128)(2,1)}, bf16[8,512,768]{2,1,0:T(8,128)(2,1)S(1)}, u32[]{:S(2)}, u32[]{:S(2)}) collective-permute-start(bf16[8,512,768]{2,1,0:T(8,128)(2,1)} %get-tuple-element.20.refs_0_), channel_id=1, source_target_pairs={{0,1},{1,0},{2,3},{3,2},{4,5},{5,4},{6,7},{7,6}} | collective-permute-start | bytes 18874376 | tf_op jit(solution)/shard_map/ppermute | solution.py:421
  729.0 367.0 %copy-start.14 = (bf16[2,512,768]{2,1,0:T(8,128)(2,1)}, bf16[2,512,768]{2,1,0:T(8,128)(2,1)S(1)}, u32[]{:S(2)}) copy-start(bf16[2,512,768]{2,1,0:T(8,128)(2,1)S(1)} %collective-permute-done.11.refs_3_) | copy-start | bytes 4718596
  729.0 367.0 %collective-permute-start.21 = (bf16[6,512,768]{2,1,0:T(8,128)(2,1)}, bf16[6,512,768]{2,1,0:T(8,128)(2,1)S(1)}, u32[]{:S(2)}, u32[]{:S(2)}) collective-permute-start(bf16[6,512,768]{2,1,0:T(8,128)(2,1)} %get-tuple-element.21.refs_0_), channel_id=1, source_target_pairs={{0,1},{1,0},{2,3},{3,2},{4,5},{5,4},{6,7},{7,6}} | collective-permute-start | bytes 14155784 | tf_op jit(solution)/shard_map/ppermute | solution.py:421
  1092.7 40.3 %copy-start.6 = (bf16[6,512,768]{2,1,0:T(8,128)(2,1)}, bf16[6,512,768]{2,1,0:T(8,128)(2,1)S(1)}, u32[]{:S(2)}) copy-start(bf16[6,512,768]{2,1,0:T(8,128)(2,1)S(1)} %collective-permute-done.22.refs_2_) | copy-start | bytes 14155780
  1092.7 10.4 collective-permute-start.15
  1092.8 2.7 copy-start
  1095.4 37.5 %collective-permute-start.20 = (bf16[8,512,768]{2,1,0:T(8,128)(2,1)S(1)}, bf16[8,512,768]{2,1,0:T(8,128)(2,1)S(1)}, u32[]{:S(2)}, u32[]{:S(2)}) collective-permute-start(bf16[8,512,768]{2,1,0:T(8,128)(2,1)S(1)} %collective-permute-done.19.refs_2_), channel_id=1, source_target_pairs={{0,1},{1,0},{2,3},{3,2},{4,5},{5,4},{6,7},{7,6}} | collective-permute-start | bytes 18874376 | tf_op jit(solution)/shard_map/ppermute | solution.py:422
  1096.0 36.9 %copy-start.1 = (bf16[8,512,768]{2,1,0:T(8,128)(2,1)}, bf16[8,512,768]{2,1,0:T(8,128)(2,1)S(1)}, u32[]{:S(2)}) copy-start(bf16[8,512,768]{2,1,0:T(8,128)(2,1)S(1)} %collective-permute-done.16.refs_2_) | copy-start | bytes 18874372
  1096.0 37.1 %collective-permute-start.17 = (bf16[8,512,768]{2,1,0:T(8,128)(2,1)S(1)}, bf16[8,512,768]{2,1,0:T(8,128)(2,1)S(1)}, u32[]{:S(2)}, u32[]{:S(2)}) collective-permute-start(bf16[8,512,768]{2,1,0:T(8,128)(2,1)S(1)} %collective-permute-done.16.refs_2_), channel_id=1, source_target_pairs={{0,1},{1,0},{2,3},{3,2},{4,5},{5,4},{6,7},{7,6}} | collective-permute-start | bytes 18874376 | tf_op jit(solution)/shard_map/ppermute | solution.py:422
  1096.0 37.0 %copy-start.7 = (bf16[6,512,768]{2,1,0:T(8,128)(2,1)}, bf16[6,512,768]{2,1,0:T(8,128)(2,1)S(1)}, u32[]{:S(2)}) copy-start(bf16[6,512,768]{2,1,0:T(8,128)(2,1)S(1)} %collective-permute-done.21.refs_1_) | copy-start | bytes 14155780
  1096.0 36.5 %collective-permute-start.23 = (bf16[6,512,768]{2,1,0:T(8,128)(2,1)S(1)}, bf16[6,512,768]{2,1,0:T(8,128)(2,1)S(1)}, u32[]{:S(2)}, u32[]{:S(2)}) collective-permute-start(bf16[6,512,768]{2,1,0:T(8,128)(2,1)S(1)} %collective-permute-done.22.refs_2_), channel_id=1, source_target_pairs={{0,1},{1,0},{2,3},{3,2},{4,5},{5,4},{6,7},{7,6}} | collective-permute-start | bytes 14155784 | tf_op jit(solution)/shard_map/ppermute | solution.py:422
  1096.5 36.5 %copy-start.2 = (bf16[8,512,768]{2,1,0:T(8,128)(2,1)}, bf16[8,512,768]{2,1,0:T(8,128)(2,1)S(1)}, u32[]{:S(2)}) copy-start(bf16[8,512,768]{2,1,0:T(8,128)(2,1)S(1)} %collective-permute-done.18.refs_1_) | copy-start | bytes 18874372
  1096.5 35.8 %collective-permute-start.14 = (bf16[4,512,768]{2,1,0:T(8,128)(2,1)S(1)}, bf16[4,512,768]{2,1,0:T(8,128)(2,1)S(1)}, u32[]{:S(2)}, u32[]{:S(2)}) collective-permute-start(bf16[4,512,768]{2,1,0:T(8,128)(2,1)S(1)} %collective-permute-done.13.refs_2_), channel_id=1, source_target_pairs={{0,1},{1,0},{2,3},{3,2},{4,5},{5,4},{6,7},{7,6}} | collective-permute-start | bytes 9437192 | tf_op jit(solution)/shard_map/ppermute | solution.py:422
  1103.1 30.0 %copy-start.3 = (bf16[8,512,768]{2,1,0:T(8,128)(2,1)}, bf16[8,512,768]{2,1,0:T(8,128)(2,1)S(1)}, u32[]{:S(2)}) copy-start(bf16[8,512,768]{2,1,0:T(8,128)(2,1)S(1)} %collective-permute-done.15.refs_1_) | copy-start | bytes 18874372
  1103.1 107.4 %collective-permute-start.6 = (bf16[1,512,768]{2,1,0:T(8,128)(2,1)}, bf16[1,512,768]{2,1,0:T(8,128)(2,1)}, u32[]{:S(2)}, u32[]{:S(2)}) collective-permute-start(bf16[1,512,768]{2,1,0:T(8,128)(2,1)} %get-tuple-element.16.refs_0_), channel_id=1, source_target_pairs={{0,1},{1,0},{2,3},{3,2},{4,5},{5,4},{6,7},{7,6}} | collective-permute-start | bytes 2359304 | tf_op jit(solution)/shard_map/ppermute | solution.py:421
  1132.4 1.7 copy-start.11
  1132.4 78.6 %collective-permute-start.8 = (bf16[1,512,768]{2,1,0:T(8,128)(2,1)}, bf16[1,512,768]{2,1,0:T(8,128)(2,1)}, u32[]{:S(2)}, u32[]{:S(2)}) collective-permute-start(bf16[1,512,768]{2,1,0:T(8,128)(2,1)} %collective-permute-done.7.refs_2_), channel_id=1, source_target_pairs={{0,1},{1,0},{2,3},{3,2},{4,5},{5,4},{6,7},{7,6}} | collective-permute-start | bytes 2359304 | tf_op jit(solution)/shard_map/ppermute | solution.py:422
  1132.5 2.9 copy-start.8
  1132.5 81.4 %collective-permute-start.5 = (bf16[1,256,768]{2,1,0:T(8,128)(2,1)}, bf16[1,256,768]{2,1,0:T(8,128)(2,1)}, u32[]{:S(2)}, u32[]{:S(2)}) collective-permute-start(bf16[1,256,768]{2,1,0:T(8,128)(2,1)} %get-tuple-element.14.refs_0_), channel_id=1, source_target_pairs={{0,1},{1,0},{2,3},{3,2},{4,5},{5,4},{6,7},{7,6}} | collective-permute-start | bytes 1179656 | tf_op jit(solution)/shard_map/ppermute | solution.py:421
  1132.9 4.5 copy-start.4
  1132.9 83.0 %collective-permute-start.2 = (bf16[1,256,768]{2,1,0:T(8,128)(2,1)}, bf16[1,256,768]{2,1,0:T(8,128)(2,1)}, u32[]{:S(2)}, u32[]{:S(2)}) collective-permute-start(bf16[1,256,768]{2,1,0:T(8,128)(2,1)} %get-tuple-element.15.refs_0_), channel_id=1, source_target_pairs={{0,1},{1,0},{2,3},{3,2},{4,5},{5,4},{6,7},{7,6}} | collective-permute-start | bytes 1179656 | tf_op jit(solution)/shard_map/ppermute | solution.py:421
  1137.4 2.7 copy-start.5
  1140.1 75.8 %collective-permute-start.4 = (bf16[1,256,768]{2,1,0:T(8,128)(2,1)}, bf16[1,256,768]{2,1,0:T(8,128)(2,1)}, u32[]{:S(2)}, u32[]{:S(2)}) collective-permute-start(bf16[1,256,768]{2,1,0:T(8,128)(2,1)} %collective-permute-done.3.refs_2_), channel_id=1, source_target_pairs={{0,1},{1,0},{2,3},{3,2},{4,5},{5,4},{6,7},{7,6}} | collective-permute-start | bytes 1179656 | tf_op jit(solution)/shard_map/ppermute | solution.py:422
  1210.5 50.7 %collective-permute-start.1 = (bf16[1,256,768]{2,1,0:T(8,128)(2,1)}, bf16[1,256,768]{2,1,0:T(8,128)(2,1)}, u32[]{:S(2)}, u32[]{:S(2)}) collective-permute-start(bf16[1,256,768]{2,1,0:T(8,128)(2,1)} %copy-done.17), channel_id=1, source_target_pairs={{0,1},{1,0},{2,3},{3,2},{4,5},{5,4},{6,7},{7,6}} | collective-permute-start | bytes 1179656 | tf_op jit(solution)/shard_map/ppermute | solution.py:422
